TPU v7x, 256 devices: a whole 4x4x8 slice. The times are simulated.
256 devices in a mesh: gx: 8 (over z_hi, core), gz: 32 (over x, z_lo, y).
Axes of the slice: x: 4, y: 4, z: 8 (z_hi: 4, z_lo: 2; z = z_hi * 2 + z_lo), core: 2. Of those that a mesh axis runs over, the one named last changes fastest.
Arguments:
- modes: bfloat16 [3, 16, 128, 256, 128], P(None, 'gx', None, 'gz'), may hold values from -6 to 6
- weights: float32 [16, 128, 256], P('gx', None, 'gz'), may hold values from 0.0007973615 to 0.007973615
- counts: int32 [256], P(('gx', 'gz')), may hold values from 1 to 128, 10922 in all
- mode_index: int32 [16], replicated, may hold values from 0 to 127, as said below
Outputs:
- slices: float32 [16, 128, 128], P(None, 'gz')
Inputs may be any that keep to these rules, and one draw needn't show every extreme that they name: `mode_index`: distinct modes. The counts sum to 128 * 8 * 32 // 3 and one pencil holds 128.
All inputs are finite; a program needn't handle non-finite values. No bound on the sum of `counts` on one device may be relied on, other than what follows from the above.
Results may differ from a plain program's by a relative error of at most 0.004.
Values may be sent and summed in bfloat16 or wider, within the bound.
A program may use at most 64 MiB of HBM per device.

v0:
```python
import jax
import jax.numpy as jnp
from jax import lax
from jax.sharding import PartitionSpec as P

YBLK = 8


def padded_2(block, sides, width):
    for axis, dim in sides:
        count = lax.axis_size(axis)
        forward = [(i, i + 1) for i in range(count - 1)]
        forward.append((count - 1, 0))
        backward = [(target, source) for source, target in forward]
        low = lax.ppermute(
            lax.slice_in_dim(block, block.shape[dim] - width, None, axis=dim), axis, forward
        )
        high = lax.ppermute(lax.slice_in_dim(block, 0, width, axis=dim), axis, backward)
        block = jnp.concatenate([low, block, high], axis=dim)
    return block


def in_blocks(value, dim, count):
    shape = value.shape
    parts = value.reshape(*shape[:dim], count, shape[dim] // count, *shape[dim + 1 :])
    return jnp.moveaxis(parts, dim, 0)


def summed_on_arrival(value, axis, dim):
    parts = in_blocks(value, dim, lax.axis_size(axis))
    arrived = lax.all_to_all(parts, axis, split_axis=0, concat_axis=0, tiled=True)
    return arrived.sum(axis=0)


def sent_to_all(value, axis):
    count = lax.axis_size(axis)
    return lax.all_to_all(
        jnp.broadcast_to(value[None], (count, *value.shape)), axis, 0, 0, tiled=True
    )


def over_copies(value, axis):
    everything = sent_to_all(value, axis)
    return jnp.sum(everything, axis=0)


def region_terms(source, weight_part, live_count, onehot, running):
    size_m = source.shape[4]
    span_x = source.shape[1] - 2
    level_cap = source.shape[2]
    span_z = source.shape[3] - 2
    points = span_x * YBLK * span_z
    highest = lax.Precision.HIGHEST
    padded = jnp.pad(source, ((0, 0), (0, 0), (1, 1), (0, 0), (0, 0)))
    levels = jnp.arange(YBLK, dtype=jnp.int32)

    def add_block(block_id, total):
        first_level = block_id * YBLK
        slab_part = lax.dynamic_slice_in_dim(padded, first_level, YBLK + 2, 2)
        centre = slab_part[:, 1:-1, 1:-1, 1:-1]
        grad_x = 0.5 * (
            slab_part[:, 2:, 1:-1, 1:-1].astype(jnp.float32)
            - slab_part[:, :-2, 1:-1, 1:-1].astype(jnp.float32)
        )
        grad_y = 0.5 * (
            slab_part[:, 1:-1, 2:, 1:-1].astype(jnp.float32)
            - slab_part[:, 1:-1, :-2, 1:-1].astype(jnp.float32)
        )
        grad_z = 0.5 * (
            slab_part[:, 1:-1, 1:-1, 2:].astype(jnp.float32)
            - slab_part[:, 1:-1, 1:-1, :-2].astype(jnp.float32)
        )
        gradient = jnp.stack([grad_x, grad_y, grad_z]).reshape(3, 3, points, size_m)
        flattened = centre.reshape(3, points, size_m)
        picked = jnp.einsum("cqm,mj->cqj", flattened, onehot, preferred_element_type=jnp.float32)
        advected = jnp.einsum("dqj,dcqk->jcqk", picked, gradient, precision=highest).astype(
            jnp.bfloat16
        )
        weight_block = lax.dynamic_slice_in_dim(weight_part, first_level, YBLK, 1)
        live_mask = (first_level + levels)[None, :, None] < live_count
        weighting = jnp.where(live_mask, weight_block, jnp.zeros_like(weight_block)).reshape(points)
        tested = (flattened.astype(jnp.float32) * weighting[None, :, None]).astype(jnp.bfloat16)
        return total + jnp.einsum(
            "cqi,jcqk->jik", tested, advected, preferred_element_type=jnp.float32
        )

    return lax.fori_loop(0, level_cap // YBLK, add_block, running)


def local(modes, weights, counts, mode_index):
    size_m = modes.shape[4]
    window = mode_index.shape[0]
    onehot = (jnp.arange(size_m)[:, None] == mode_index[None, :]).astype(jnp.bfloat16)
    live_count = counts[0]
    extended = padded_2(modes, (("gx", 1), ("gz", 3)), 1)
    running = jnp.zeros((window, size_m, size_m), jnp.float32)
    running = region_terms(extended, weights, live_count, onehot, running)
    partial_sum = summed_on_arrival(running, "gz", 1)
    owned = over_copies(partial_sum, "gx")
    return owned


def solution(mesh):
    placed = (P(None, "gx", None, "gz", None), P("gx", None, "gz"), P(("gx", "gz")), P())
    return jax.shard_map(
        local, mesh=mesh, in_specs=placed, out_specs=P(None, "gz", None), check_vma=False
    )
```

profile of v0, /device:TPU:1, one launch (start us, length us, event | category | flops | bytes accessed | tf_op | source)
XLA Modules:
  0.0 245.5 jit_solution(17051919219563621780)
XLA Ops:
  0.0 1.5 fusion.34
  1.7 4.4 %collective-permute-start = (bf16[3,1,128,8,128]{4,2,3,1,0:T(8,128)(2,1)S(1)}, bf16[3,1,128,8,128]{4,2,3,1,0:T(8,128)(2,1)S(1)}, u32[]{:S(2)}, u32[]{:S(2)}) collective-permute-start(bf16[3,1,128,8,128]{4,2,3,1,0:T(8,128)(2,1)S(1)} %copy.70), channel_id=1, source_target_pairs={{0,32},{32,64},{64,96},{96,128},{128,160},{160,192},{192,224},{224... | collective-permute-start | bytes 2359304 | tf_op jit(solution)/shard_map/ppermute | solution.py:15
  6.4 11.1 %collective-permute-done = bf16[3,1,128,8,128]{4,2,3,1,0:T(8,128)(2,1)S(1)} collective-permute-done((bf16[3,1,128,8,128]{4,2,3,1,0:T(8,128)(2,1)S(1)}, bf16[3,1,128,8,128]{4,2,3,1,0:T(8,128)(2,1)S(1)}, u32[]{:S(2)}, u32[]{:S(2)}) %collective-permute-start) | collective-permute-done | bytes 786464 | tf_op jit(solution)/shard_map/ppermute | solution.py:15
  18.1 9.1 %collective-permute-done.1 = bf16[3,1,128,8,128]{4,2,3,1,0:T(8,128)(2,1)S(1)} collective-permute-done((bf16[3,1,128,8,128]{4,2,3,1,0:T(8,128)(2,1)S(1)}, bf16[3,1,128,8,128]{4,2,3,1,0:T(8,128)(2,1)S(1)}, u32[]{:S(2)}, u32[]{:S(2)}) %collective-permute-start.1) | collective-permute-done | bytes 786464 | tf_op jit(solution)/shard_map/ppermute | solution.py:18
  27.4 1.4 collective-permute-start.2
  29.0 4.2 %collective-permute-start.3 = (bf16[3,4,128,1,128]{4,2,3,1,0:T(8,128)(2,1)S(1)}, bf16[3,4,128,1,128]{4,2,3,1,0:T(8,128)(2,1)S(1)}, u32[]{:S(2)}, u32[]{:S(2)}) collective-permute-start(bf16[3,4,128,1,128]{4,2,3,1,0:T(8,128)(2,1)S(1)} %get-tuple-element.208), channel_id=1, source_target_pairs={{1,0},{2,1},{3,2},{4,3},{5,4},{6,5},{7,6},{8,7},{9,8},{10,9},{11,1... | collective-permute-start | bytes 1179656 | tf_op jit(solution)/shard_map/ppermute | solution.py:18
  33.2 9.2 %collective-permute-done.2 = bf16[3,4,128,1,128]{4,2,3,1,0:T(8,128)(2,1)S(1)} collective-permute-done((bf16[3,4,128,1,128]{4,2,3,1,0:T(8,128)(2,1)S(1)}, bf16[3,4,128,1,128]{4,2,3,1,0:T(8,128)(2,1)S(1)}, u32[]{:S(2)}, u32[]{:S(2)}) %collective-permute-start.2) | collective-permute-done | bytes 393248 | tf_op jit(solution)/shard_map/ppermute | solution.py:15
  42.4 4.5 %fusion.32 = bf16[3,4,130,10,128]{4,2,3,1,0:T(8,128)(2,1)} fusion(bf16[3,4,128,1,128]{4,2,3,1,0:T(8,128)(2,1)S(1)} %collective-permute-done.3, bf16[3,4,128,8,128]{4,2,3,1,0:T(8,128)(2,1)} %copy-done, bf16[3,4,128,1,128]{4,2,3,1,0:T(8,128)(2,1)S(1)} %collective-permute-done.2), kind=kLoop, calls=%fused_computation.43 | loop fusion | flops 23961600 | bytes 7925760 | tf_op jit(solution)/shard_map/concatenate | solution.py:19
  46.9 156.0 %while.14 = (s32[]{:T(128)}, f32[16,128,128]{1,2,0:T(8,128)S(1)}, bf16[3,4,130,10,128]{4,2,3,1,0:T(8,128)(2,1)}, s32[]{:T(128)}, f32[2,128,8]{1,2,0:T(8,128)S(1)...) while((s32[]{:T(128)}, f32[16,128,128]{1,2,0:T(8,128)S(1)}, ...), condition=%wide.region_1.2_spmd.clone, body=%wide.region_0.1_spmd.clone.sunk | while | flops 233558176 | bytes 10064750 | solution.py:87
  46.9 1.8 constant_dynamic-slice_fusion.10
  49.2 0.9 copy.91
  50.5 4.1 %fusion.52 = bf16[16,3,128,128]{3,0,1,2:T(8,128)(2,1)S(1)} fusion(f32[3,128,16,1]{2,0,3,1:T(4,128)S(1)} %copy.89, f32[1,3,128,128]{3,0,1,2:T(1,128)S(1)} %copy.90, f32[1,3,128,128]{3,0,1,2:T(1,128)} %copy.91, f32[1,3,128,128]{3,0,1,2:T(1,128)S(1)} %copy.92), kind=kOutput, calls=%fused_computation.5.clone.1 | convolution fusion | flops 29392896 | bytes 2187264 | tf_op jit(solution)/shard_map/while/body/eval_jaxpr/dqj,dcqk->jcqk/dot_general | solution.py:76
  55.5 1.0 fusion.54
  56.6 2.0 constant_dynamic-slice_fusion.10
  59.1 0.9 copy.91
  60.3 4.1 %fusion.52 = bf16[16,3,128,128]{3,0,1,2:T(8,128)(2,1)S(1)} fusion(f32[3,128,16,1]{2,0,3,1:T(4,128)S(1)} %copy.89, f32[1,3,128,128]{3,0,1,2:T(1,128)S(1)} %copy.90, f32[1,3,128,128]{3,0,1,2:T(1,128)} %copy.91, f32[1,3,128,128]{3,0,1,2:T(1,128)S(1)} %copy.92), kind=kOutput, calls=%fused_computation.5.clone.1 | convolution fusion | flops 29392896 | bytes 2187264 | tf_op jit(solution)/shard_map/while/body/eval_jaxpr/dqj,dcqk->jcqk/dot_general | solution.py:76
  65.4 1.0 fusion.54
  66.4 1.9 constant_dynamic-slice_fusion.10
  68.8 0.9 copy.91
  70.1 4.1 %fusion.52 = bf16[16,3,128,128]{3,0,1,2:T(8,128)(2,1)S(1)} fusion(f32[3,128,16,1]{2,0,3,1:T(4,128)S(1)} %copy.89, f32[1,3,128,128]{3,0,1,2:T(1,128)S(1)} %copy.90, f32[1,3,128,128]{3,0,1,2:T(1,128)} %copy.91, f32[1,3,128,128]{3,0,1,2:T(1,128)S(1)} %copy.92), kind=kOutput, calls=%fused_computation.5.clone.1 | convolution fusion | flops 29392896 | bytes 2187264 | tf_op jit(solution)/shard_map/while/body/eval_jaxpr/dqj,dcqk->jcqk/dot_general | solution.py:76
  75.1 1.0 fusion.54
  76.2 1.8 constant_dynamic-slice_fusion.10
  78.5 0.9 copy.91
  79.8 4.1 %fusion.52 = bf16[16,3,128,128]{3,0,1,2:T(8,128)(2,1)S(1)} fusion(f32[3,128,16,1]{2,0,3,1:T(4,128)S(1)} %copy.89, f32[1,3,128,128]{3,0,1,2:T(1,128)S(1)} %copy.90, f32[1,3,128,128]{3,0,1,2:T(1,128)} %copy.91, f32[1,3,128,128]{3,0,1,2:T(1,128)S(1)} %copy.92), kind=kOutput, calls=%fused_computation.5.clone.1 | convolution fusion | flops 29392896 | bytes 2187264 | tf_op jit(solution)/shard_map/while/body/eval_jaxpr/dqj,dcqk->jcqk/dot_general | solution.py:76
  84.9 1.0 fusion.54
  85.9 1.9 constant_dynamic-slice_fusion.10
  88.4 0.9 copy.91
  89.6 4.1 %fusion.52 = bf16[16,3,128,128]{3,0,1,2:T(8,128)(2,1)S(1)} fusion(f32[3,128,16,1]{2,0,3,1:T(4,128)S(1)} %copy.89, f32[1,3,128,128]{3,0,1,2:T(1,128)S(1)} %copy.90, f32[1,3,128,128]{3,0,1,2:T(1,128)} %copy.91, f32[1,3,128,128]{3,0,1,2:T(1,128)S(1)} %copy.92), kind=kOutput, calls=%fused_computation.5.clone.1 | convolution fusion | flops 29392896 | bytes 2187264 | tf_op jit(solution)/shard_map/while/body/eval_jaxpr/dqj,dcqk->jcqk/dot_general | solution.py:76
  94.7 1.0 fusion.54
  95.7 1.8 constant_dynamic-slice_fusion.10
  99.3 4.1 %fusion.52 = bf16[16,3,128,128]{3,0,1,2:T(8,128)(2,1)S(1)} fusion(f32[3,128,16,1]{2,0,3,1:T(4,128)S(1)} %copy.89, f32[1,3,128,128]{3,0,1,2:T(1,128)S(1)} %copy.90, f32[1,3,128,128]{3,0,1,2:T(1,128)} %copy.91, f32[1,3,128,128]{3,0,1,2:T(1,128)S(1)} %copy.92), kind=kOutput, calls=%fused_computation.5.clone.1 | convolution fusion | flops 29392896 | bytes 2187264 | tf_op jit(solution)/shard_map/while/body/eval_jaxpr/dqj,dcqk->jcqk/dot_general | solution.py:76
  104.3 1.0 fusion.54
  105.4 1.9 constant_dynamic-slice_fusion.10
  109.0 4.1 %fusion.52 = bf16[16,3,128,128]{3,0,1,2:T(8,128)(2,1)S(1)} fusion(f32[3,128,16,1]{2,0,3,1:T(4,128)S(1)} %copy.89, f32[1,3,128,128]{3,0,1,2:T(1,128)S(1)} %copy.90, f32[1,3,128,128]{3,0,1,2:T(1,128)} %copy.91, f32[1,3,128,128]{3,0,1,2:T(1,128)S(1)} %copy.92), kind=kOutput, calls=%fused_computation.5.clone.1 | convolution fusion | flops 29392896 | bytes 2187264 | tf_op jit(solution)/shard_map/while/body/eval_jaxpr/dqj,dcqk->jcqk/dot_general | solution.py:76
  114.1 1.0 fusion.54
  115.1 1.8 constant_dynamic-slice_fusion.10
  118.7 4.1 %fusion.52 = bf16[16,3,128,128]{3,0,1,2:T(8,128)(2,1)S(1)} fusion(f32[3,128,16,1]{2,0,3,1:T(4,128)S(1)} %copy.89, f32[1,3,128,128]{3,0,1,2:T(1,128)S(1)} %copy.90, f32[1,3,128,128]{3,0,1,2:T(1,128)} %copy.91, f32[1,3,128,128]{3,0,1,2:T(1,128)S(1)} %copy.92), kind=kOutput, calls=%fused_computation.5.clone.1 | convolution fusion | flops 29392896 | bytes 2187264 | tf_op jit(solution)/shard_map/while/body/eval_jaxpr/dqj,dcqk->jcqk/dot_general | solution.py:76
  123.8 1.0 fusion.54
  124.8 1.9 constant_dynamic-slice_fusion.10
  128.5 4.1 %fusion.52 = bf16[16,3,128,128]{3,0,1,2:T(8,128)(2,1)S(1)} fusion(f32[3,128,16,1]{2,0,3,1:T(4,128)S(1)} %copy.89, f32[1,3,128,128]{3,0,1,2:T(1,128)S(1)} %copy.90, f32[1,3,128,128]{3,0,1,2:T(1,128)} %copy.91, f32[1,3,128,128]{3,0,1,2:T(1,128)S(1)} %copy.92), kind=kOutput, calls=%fused_computation.5.clone.1 | convolution fusion | flops 29392896 | bytes 2187264 | tf_op jit(solution)/shard_map/while/body/eval_jaxpr/dqj,dcqk->jcqk/dot_general | solution.py:76
  133.6 1.0 fusion.54
  134.6 1.9 constant_dynamic-slice_fusion.10
  138.3 4.1 %fusion.52 = bf16[16,3,128,128]{3,0,1,2:T(8,128)(2,1)S(1)} fusion(f32[3,128,16,1]{2,0,3,1:T(4,128)S(1)} %copy.89, f32[1,3,128,128]{3,0,1,2:T(1,128)S(1)} %copy.90, f32[1,3,128,128]{3,0,1,2:T(1,128)} %copy.91, f32[1,3,128,128]{3,0,1,2:T(1,128)S(1)} %copy.92), kind=kOutput, calls=%fused_computation.5.clone.1 | convolution fusion | flops 29392896 | bytes 2187264 | tf_op jit(solution)/shard_map/while/body/eval_jaxpr/dqj,dcqk->jcqk/dot_general | solution.py:76
  143.4 1.0 fusion.54
  144.4 2.0 constant_dynamic-slice_fusion.10
  148.2 4.1 %fusion.52 = bf16[16,3,128,128]{3,0,1,2:T(8,128)(2,1)S(1)} fusion(f32[3,128,16,1]{2,0,3,1:T(4,128)S(1)} %copy.89, f32[1,3,128,128]{3,0,1,2:T(1,128)S(1)} %copy.90, f32[1,3,128,128]{3,0,1,2:T(1,128)} %copy.91, f32[1,3,128,128]{3,0,1,2:T(1,128)S(1)} %copy.92), kind=kOutput, calls=%fused_computation.5.clone.1 | convolution fusion | flops 29392896 | bytes 2187264 | tf_op jit(solution)/shard_map/while/body/eval_jaxpr/dqj,dcqk->jcqk/dot_general | solution.py:76
  153.3 1.0 fusion.54
  154.3 1.8 constant_dynamic-slice_fusion.10
  157.9 4.1 %fusion.52 = bf16[16,3,128,128]{3,0,1,2:T(8,128)(2,1)S(1)} fusion(f32[3,128,16,1]{2,0,3,1:T(4,128)S(1)} %copy.89, f32[1,3,128,128]{3,0,1,2:T(1,128)S(1)} %copy.90, f32[1,3,128,128]{3,0,1,2:T(1,128)} %copy.91, f32[1,3,128,128]{3,0,1,2:T(1,128)S(1)} %copy.92), kind=kOutput, calls=%fused_computation.5.clone.1 | convolution fusion | flops 29392896 | bytes 2187264 | tf_op jit(solution)/shard_map/while/body/eval_jaxpr/dqj,dcqk->jcqk/dot_general | solution.py:76
  163.0 1.0 fusion.54
  164.0 1.9 constant_dynamic-slice_fusion.10
  167.6 4.1 %fusion.52 = bf16[16,3,128,128]{3,0,1,2:T(8,128)(2,1)S(1)} fusion(f32[3,128,16,1]{2,0,3,1:T(4,128)S(1)} %copy.89, f32[1,3,128,128]{3,0,1,2:T(1,128)S(1)} %copy.90, f32[1,3,128,128]{3,0,1,2:T(1,128)} %copy.91, f32[1,3,128,128]{3,0,1,2:T(1,128)S(1)} %copy.92), kind=kOutput, calls=%fused_computation.5.clone.1 | convolution fusion | flops 29392896 | bytes 2187264 | tf_op jit(solution)/shard_map/while/body/eval_jaxpr/dqj,dcqk->jcqk/dot_general | solution.py:76
  172.7 1.0 fusion.54
  173.8 2.0 constant_dynamic-slice_fusion.10
  177.6 4.1 %fusion.52 = bf16[16,3,128,128]{3,0,1,2:T(8,128)(2,1)S(1)} fusion(f32[3,128,16,1]{2,0,3,1:T(4,128)S(1)} %copy.89, f32[1,3,128,128]{3,0,1,2:T(1,128)S(1)} %copy.90, f32[1,3,128,128]{3,0,1,2:T(1,128)} %copy.91, f32[1,3,128,128]{3,0,1,2:T(1,128)S(1)} %copy.92), kind=kOutput, calls=%fused_computation.5.clone.1 | convolution fusion | flops 29392896 | bytes 2187264 | tf_op jit(solution)/shard_map/while/body/eval_jaxpr/dqj,dcqk->jcqk/dot_general | solution.py:76
  182.6 1.0 fusion.54
  183.7 1.7 constant_dynamic-slice_fusion.10
  187.2 4.1 %fusion.52 = bf16[16,3,128,128]{3,0,1,2:T(8,128)(2,1)S(1)} fusion(f32[3,128,16,1]{2,0,3,1:T(4,128)S(1)} %copy.89, f32[1,3,128,128]{3,0,1,2:T(1,128)S(1)} %copy.90, f32[1,3,128,128]{3,0,1,2:T(1,128)} %copy.91, f32[1,3,128,128]{3,0,1,2:T(1,128)S(1)} %copy.92), kind=kOutput, calls=%fused_computation.5.clone.1 | convolution fusion | flops 29392896 | bytes 2187264 | tf_op jit(solution)/shard_map/while/body/eval_jaxpr/dqj,dcqk->jcqk/dot_general | solution.py:76
  192.2 1.0 fusion.54
  193.3 1.8 constant_dynamic-slice_fusion.10
  196.8 4.1 %fusion.52 = bf16[16,3,128,128]{3,0,1,2:T(8,128)(2,1)S(1)} fusion(f32[3,128,16,1]{2,0,3,1:T(4,128)S(1)} %copy.89, f32[1,3,128,128]{3,0,1,2:T(1,128)S(1)} %copy.90, f32[1,3,128,128]{3,0,1,2:T(1,128)} %copy.91, f32[1,3,128,128]{3,0,1,2:T(1,128)S(1)} %copy.92), kind=kOutput, calls=%fused_computation.5.clone.1 | convolution fusion | flops 29392896 | bytes 2187264 | tf_op jit(solution)/shard_map/while/body/eval_jaxpr/dqj,dcqk->jcqk/dot_general | solution.py:76
  201.9 1.0 fusion.54
  203.4 20.5 %all_to_all.10 = f32[32,16,4,128]{3,1,2,0:T(8,128)S(1)} all-to-all(f32[32,16,4,128]{3,1,2,0:T(8,128)S(1)} %bitcast.54), channel_id=1, replica_groups=mesh['gx'=8,'gz'=32] {'gz'}, dimensions={0} | all-to-all | bytes 2097152 | tf_op jit(solution)/shard_map/all_to_all | solution.py:31
  224.0 20.9 %all_to_all.11 = f32[8,16,4,128]{3,1,2,0:T(8,128)S(1)} all-to-all(f32[8,16,4,128]{3,1,2,0:T(8,128)S(1)} %broadcast_in_dim.33), channel_id=1, replica_groups=mesh['gx'=8,'gz'=32] {'gx'}, dimensions={0} | all-to-all | bytes 524288 | tf_op jit(solution)/shard_map/all_to_all | solution.py:37
  (225 shorter events, 41.2 us)
Async XLA Ops:
  1.5 16.0 %copy-start.1 = (bf16[3,2,128,8,128]{4,3,2,1,0:T(8,128)(2,1)S(1)}, bf16[3,2,128,8,128]{4,3,2,1,0:T(8,128)(2,1)}, u32[]{:S(2)}) copy-start(bf16[3,2,128,8,128]{4,3,2,1,0:T(8,128)(2,1)} %param.6) | copy-start | bytes 4718596
  1.7 15.8 %collective-permute-start = (bf16[3,1,128,8,128]{4,2,3,1,0:T(8,128)(2,1)S(1)}, bf16[3,1,128,8,128]{4,2,3,1,0:T(8,128)(2,1)S(1)}, u32[]{:S(2)}, u32[]{:S(2)}) collective-permute-start(bf16[3,1,128,8,128]{4,2,3,1,0:T(8,128)(2,1)S(1)} %copy.70), channel_id=1, source_target_pairs={{0,32},{32,64},{64,96},{96,128},{128,160},{160,192},{192,224},{224... | collective-permute-start | bytes 2359304 | tf_op jit(solution)/shard_map/ppermute | solution.py:15
  6.3 20.9 %collective-permute-start.1 = (bf16[3,1,128,8,128]{4,2,3,1,0:T(8,128)(2,1)S(1)}, bf16[3,1,128,8,128]{4,2,3,1,0:T(8,128)(2,1)S(1)}, u32[]{:S(2)}, u32[]{:S(2)}) collective-permute-start(bf16[3,1,128,8,128]{4,2,3,1,0:T(8,128)(2,1)S(1)} %copy.71), channel_id=1, source_target_pairs={{32,0},{64,32},{96,64},{128,96},{160,128},{192,160},{224,192},{0,2... | collective-permute-start | bytes 2359304 | tf_op jit(solution)/shard_map/ppermute | solution.py:18
  27.3 1.7 copy-start
  27.4 15.0 %collective-permute-start.2 = (bf16[3,4,128,1,128]{4,2,3,1,0:T(8,128)(2,1)S(1)}, bf16[3,4,128,1,128]{4,2,3,1,0:T(8,128)(2,1)S(1)}, u32[]{:S(2)}, u32[]{:S(2)}) collective-permute-start(bf16[3,4,128,1,128]{4,2,3,1,0:T(8,128)(2,1)S(1)} %get-tuple-element.207), channel_id=1, source_target_pairs={{0,1},{1,2},{2,3},{3,4},{4,5},{5,6},{6,7},{7,8},{8,9},{9,10},{10,1... | collective-permute-start | bytes 1179656 | tf_op jit(solution)/shard_map/ppermute | solution.py:15
  29.0 13.4 %collective-permute-start.3 = (bf16[3,4,128,1,128]{4,2,3,1,0:T(8,128)(2,1)S(1)}, bf16[3,4,128,1,128]{4,2,3,1,0:T(8,128)(2,1)S(1)}, u32[]{:S(2)}, u32[]{:S(2)}) collective-permute-start(bf16[3,4,128,1,128]{4,2,3,1,0:T(8,128)(2,1)S(1)} %get-tuple-element.208), channel_id=1, source_target_pairs={{1,0},{2,1},{3,2},{4,3},{5,4},{6,5},{7,6},{8,7},{9,8},{10,9},{11,1... | collective-permute-start | bytes 1179656 | tf_op jit(solution)/shard_map/ppermute | solution.py:18
  33.2 13.7 %copy-start.2 = (f32[2,128,8]{1,2,0:T(8,128)S(1)}, f32[2,128,8]{1,2,0:T(8,128)}, u32[]{:S(2)}) copy-start(f32[2,128,8]{1,2,0:T(8,128)} %param.7) | copy-start | bytes 24580
  33.2 13.7 %copy-start.3 = (s32[16]{0:T(128)S(1)}, s32[16]{0:T(128)}, u32[]{:S(2)}) copy-start(s32[16]{0:T(128)} %param.9) | copy-start | bytes 196
where the time goes:
time: 249 us; the launch traced here: 246 us
  matrix products  84.1 us (34%)
  local copies, waits for them, and re-layouts  61.1 us (25%)
  blocking collectives  41.4 us (17%)
  waiting for transfers between devices  29.4 us (12%)
  other arithmetic  17.6 us (7%)
  starting transfers between devices  10.1 us (4%)
    dot_general x16, matrix products, add_block(): jnp.einsum('dqj,dcqk->jcqk', picked, gradient, precision=highest)  65.3 us
    slice x16, local copies, waits for them, and re-layouts, add_block(): slab_part[:, 2:, 1:-1, 1:-1].astype(jnp.float32)  30 us
    all_to_all x1, blocking collectives, sent_to_all(): lax.all_to_all(jnp.broadcast_to(value[None], (count, *value.shape)), axis...  20.9 us
    another operation x48, local copies, waits for them, and re-layouts, add_block(): gradient = jnp.stack([grad_x, grad_y, grad_z]).reshape(3, 3, points, size_m)  20.5 us
    all_to_all x1, blocking collectives, summed_on_arrival(): lax.all_to_all(parts, axis, split_axis=0, concat_axis=0, tiled=True)  20.5 us
    ppermute x2, waiting for transfers between devices, padded_2(): lax.ppermute(lax.slice_in_dim(block, block.shape[dim] - width, None, axis...  20.3 us
    dot_general x16, matrix products, add_block(): jnp.einsum('cqi,jcqk->jik', tested, advected, preferred_element_type=jnp....  16 us
    lt x16, other arithmetic, add_block(): live_mask = (first_level + levels)[None, :, None] < live_count  10.5 us
  transfers between devices with their start and end apart: 4, of which 3 were waited for; matrix products, arithmetic and copies ran while one was open for 0% of the time, Pallas kernels for 0%

commit v1 on v0

v1 whole, which is shorter than its diff:
```python
import functools

import jax
import jax.numpy as jnp
from jax import lax
from jax.experimental import pallas as pl
from jax.experimental.pallas import tpu as pltpu
from jax.sharding import PartitionSpec as P

MESH = pl.DeviceIdType.MESH
BF = jnp.bfloat16
F32 = jnp.float32
M = 128
JW = 16
LV = 128
CZ = 8
ROWS = LV * CZ
PAD = 16
CH = 128
PT = 2 * CH
GRP = 32
STEPS = PT // GRP
HALF = ROWS // 2


def iota(shape, dim):
    return lax.broadcasted_iota(jnp.int32, shape, dim)


def pick_matrix(idx_ref, scales):
    lane = iota((1, M), 1)
    wanted = jnp.zeros((1, M), jnp.int32)
    for j in range(JW):
        wanted = jnp.where(lane % JW == j, idx_ref[j], wanted)
    wanted = jnp.broadcast_to(wanted, (M, M))
    row, col = iota((M, M), 0), iota((M, M), 1)
    blocks = []
    for d, scale in enumerate(scales):
        hit = (row == wanted) & (col // JW == d)
        blocks.append(jnp.where(hit, scale, 0.0).astype(BF))
    return blocks


def weighted_columns(sw, first):
    return jnp.concatenate(
        [jnp.broadcast_to(sw[:, y : y + 1], (CZ, M)) for y in range(first, first + CH // CZ)], axis=0
    )


def dot_part(total, tested, spread, step):
    cols = pl.ds(pl.multiple_of(step * 256, 256), 256)
    total[:, cols] += jnp.dot(tested[...], spread[:, cols], preferred_element_type=F32)


def run_chunks(total, tested, spread, prepare, terms, count):
    for k in range(count + 1):
        if k < count:
            prepare(k, tested[k % 2])

        def step(s, carry, k=k):
            if k > 0:
                dot_part(total, tested[(k - 1) % 2], spread[(k - 1) % 2], s)
            if k < count:
                terms(s, spread[k % 2])
            return carry

        lax.fori_loop(0, STEPS, step, 0)


def local_kernel(
    modes, near, zlo, zhi, sw, idx, total, planes, grad, picks, stencil, sel, tt0, tt1, sp0, sp1, sems
):
    odd = lax.rem(lax.axis_index("gx"), 2)
    sign = jnp.where(odd == 0, 0.5, -0.5).astype(F32)
    copies = []
    for c in range(3):
        for side in range(2):
            which = odd if side == 0 else 1 - odd
            copies.append(
                pltpu.make_async_copy(
                    modes.at[c, which], planes.at[c, side, pl.ds(PAD, ROWS)], sems.at[2 * c + side]
                )
            )
            copies[-1].start()
    for c in range(3):
        for side in range(2):
            planes[c, side, pl.ds(0, PAD), :] = jnp.zeros((PAD, M), BF)
            planes[c, side, pl.ds(PAD + ROWS, PAD), :] = jnp.zeros((PAD, M), BF)
    row, col = iota((2 * CH, 2 * CH), 0), iota((2 * CH, 2 * CH), 1)
    point = lax.rem(row, CH)
    lev, z = point // CZ, lax.rem(point, CZ)
    here = point + PAD
    in_y = jnp.where(col == here + CZ, 1.0, 0.0) - jnp.where(col == here - CZ, 1.0, 0.0)
    ahead = jnp.where(z < CZ - 1, here + 1, 2 * PAD + CH + 16 + lev)
    behind = jnp.where(z > 0, here - 1, 2 * PAD + CH + lev)
    in_z = jnp.where(col == ahead, 1.0, 0.0) - jnp.where(col == behind, 1.0, 0.0)
    stencil[...] = jnp.where(row < CH, in_y, in_z).astype(BF)
    for d, block in enumerate(pick_matrix(idx, (sign, 0.5, 0.5))):
        sel[d * M : (d + 1) * M, :] = block
    total[...] = jnp.zeros_like(total)
    for copy in copies:
        copy.wait()

    def prepare(k, tested):
        first = k * CH
        for side in range(2):
            which = odd if side == 0 else 1 - odd
            wide = weighted_columns(sw[which], k * (CH // CZ))
            rows = slice(side * CH, (side + 1) * CH)
            mine = []
            for c in range(3):
                window = planes[c, side, first : first + CH + 2 * PAD, :]
                lo = zlo[c, which, k * 16 : (k + 1) * 16, :]
                hi = zhi[c, which, k * 16 : (k + 1) * 16, :]
                stacked = jnp.concatenate([window, lo, hi, jnp.zeros((64, M), BF)], axis=0)
                both = jnp.dot(stencil[...], stacked, preferred_element_type=F32)
                grad[3 + c, rows, :] = both[:CH]
                grad[6 + c, rows, :] = both[CH:]
                here = window[PAD : PAD + CH]
                mine.append(here)
                here = here.astype(F32)
                other = planes[c, 1 - side, PAD + first : PAD + first + CH, :].astype(F32)
                if side == 0:
                    grad[c, rows, :] = other
                else:
                    grad[c, rows, :] = near[c, first : first + CH, :].astype(F32) - other
                at = c * PT + side * CH
                tested[:, at : at + CH] = (here * wide).T.astype(BF)
            picks[rows, :] = jnp.dot(jnp.concatenate(mine, axis=1), sel[...], preferred_element_type=F32)

    def terms(s, spread):
        rows = pl.ds(pl.multiple_of(s * GRP, GRP), GRP)
        pk = picks[rows, :]
        g = [grad[q, rows, :] for q in range(9)]
        for j in range(JW):
            px, py, pz = [jnp.broadcast_to(pk[:, d * JW + j : d * JW + j + 1], (GRP, M)) for d in range(3)]
            for c in range(3):
                value = px * g[c] + py * g[3 + c] + pz * g[6 + c]
                at = pl.ds(pl.multiple_of(c * PT + s * GRP, GRP), GRP)
                spread[at, j * M : (j + 1) * M] = value.astype(BF)

    run_chunks(total, (tt0, tt1), (sp0, sp1), prepare, terms, ROWS // CH)


def cross_kernel(
    total_in, mine, far, sw, swfar, idx, out, total, vals, picks, selp, seln, tt0, tt1, sp0, sp1
):
    odd = lax.rem(lax.axis_index("gx"), 2)
    sign = jnp.where(odd == 0, 0.5, -0.5).astype(F32)
    selp[...] = pick_matrix(idx, (sign,))[0]
    seln[...] = pick_matrix(idx, (-sign,))[0]
    total[...] = total_in[...]

    def prepare(k, tested):
        first = (k % 2) * PT
        own = k < 2
        tsrc, vsrc, w, sel = (mine, far, sw, seln) if own else (far, mine, swfar, selp)
        wide = jnp.concatenate(
            [weighted_columns(w[...], (k % 2) * 32), weighted_columns(w[...], (k % 2) * 32 + 16)], axis=0
        )
        for c in range(3):
            here = tsrc[c, first : first + PT, :]
            if c == 0:
                picks[...] = jnp.dot(here, sel[...], preferred_element_type=F32)
            tested[:, c * PT : (c + 1) * PT] = (here.astype(F32) * wide).T.astype(BF)
            vals[c] = vsrc[c, first : first + PT, :].astype(F32)

    def terms(s, spread):
        rows = pl.ds(pl.multiple_of(s * GRP, GRP), GRP)
        pk = picks[rows, :]
        v = [vals[c, rows, :] for c in range(3)]
        for j in range(JW):
            px = jnp.broadcast_to(pk[:, j : j + 1], (GRP, M))
            for c in range(3):
                at = pl.ds(pl.multiple_of(c * PT + s * GRP, GRP), GRP)
                spread[at, j * M : (j + 1) * M] = (px * v[c]).astype(BF)

    run_chunks(total, (tt0, tt1), (sp0, sp1), prepare, terms, 4)
    for q in range(16):
        for low in range(2):
            owner = (q // 4) * 8 + low * 4 + q % 4
            out[q, low * 4 : low * 4 + 4, :] = total[owner * 4 : owner * 4 + 4, :]


def reduce_kernel(part, out, pair, send, got, column, stack, whole, asend, arecv, bsend, brecv, csend, crecv, dsem):
    gx, gz = lax.axis_index("gx"), lax.axis_index("gz")
    core, zh = lax.rem(gx, 2), gx // 2
    x, low, y = gz // 8, lax.rem(gz // 4, 2), lax.rem(gz, 4)
    q, z = x * 4 + y, zh * 2 + low
    partner = (gx + 1 - 2 * core, gz)

    def plane_peer(p):
        return (gx, (p // 4) * 8 + low * 4 + lax.rem(p, 4))

    def column_peer(p):
        return ((p // 2) * 2 + core, x * 8 + lax.rem(p, 2) * 4 + y)

    barrier = pltpu.get_barrier_semaphore()
    peers = [partner]
    peers += [plane_peer(lax.rem(q + d, 16)) for d in range(1, 16)]
    peers += [column_peer(lax.rem(z + d, 8)) for d in range(1, 8)]
    for peer in peers:
        pl.semaphore_signal(barrier, inc=1, device_id=peer, device_id_type=MESH)
    pl.semaphore_wait(barrier, len(peers))

    width = 8 * M
    own = pl.ds(pl.multiple_of(core * width, width), width)
    theirs = pl.ds(pl.multiple_of((1 - core) * width, width), width)

    def pair_copy(g):
        quarter = pl.ds(g * 4, 4)
        return pltpu.make_async_remote_copy(
            src_ref=part.at[quarter, :, theirs],
            dst_ref=pair.at[quarter],
            send_sem=asend.at[g],
            recv_sem=arecv.at[g],
            device_id=partner,
            device_id_type=MESH,
        )

    def plane_copy(dest, slot):
        return pltpu.make_async_remote_copy(
            src_ref=send.at[dest],
            dst_ref=got.at[slot],
            send_sem=bsend.at[dest],
            recv_sem=brecv.at[slot],
            device_id=plane_peer(dest),
            device_id_type=MESH,
        )

    def column_copy(dest, slot):
        return pltpu.make_async_remote_copy(
            src_ref=column.at[lax.rem(dest, 2)],
            dst_ref=stack.at[slot],
            send_sem=csend.at[dest],
            recv_sem=crecv.at[slot],
            device_id=column_peer(dest),
            device_id_type=MESH,
        )

    for g in range(4):
        pair_copy(g).start()
    for g in range(4):
        pair_copy(g).wait_recv()
        for b in range(g * 4, g * 4 + 4):
            send[b] = (part[b, :, own] + pair[b]).astype(BF)

            @pl.when(b != q)
            def _(b=b):
                plane_copy(b, q).start()

    total = send[q].astype(F32)
    for d in range(1, 16):
        p = lax.rem(q + d, 16)
        plane_copy(p, p).wait_recv()
        total = total + got[p].astype(F32)
    column[0] = total[:4]
    column[1] = total[4:]
    for d in (4, 3, 5, 2, 6, 1, 7):
        column_copy(lax.rem(z + d, 8), z).start()
    stack[z] = column[low]
    for d in range(1, 8):
        p = lax.rem(z + d, 8)
        column_copy(p, p).wait_recv()
    mine = stack[0]
    for p in range(1, 8):
        mine = mine + stack[p]
    for j in range(8):
        whole[core * 8 + j] = mine[:, j * M : (j + 1) * M]
    block = whole.at[pl.ds(core * 8, 8)]
    last = pltpu.make_async_remote_copy(
        src_ref=block, dst_ref=block, send_sem=dsem.at[0], recv_sem=dsem.at[1],
        device_id=partner, device_id_type=MESH,
    )
    last.start()
    for g in range(4):
        pair_copy(g).wait_send()
    for d in range(1, 16):
        plane_copy(lax.rem(q + d, 16), q).wait_send()
    for d in range(1, 8):
        column_copy(lax.rem(z + d, 8), z).wait_send()
    last.wait()
    out[...] = whole[...]


VM = pl.BlockSpec(memory_space=pltpu.VMEM)
SM = pl.BlockSpec(memory_space=pltpu.SMEM)
HB = pl.BlockSpec(memory_space=pl.ANY)


def buffers():
    return [pltpu.VMEM((M, 3 * PT), BF)] * 2 + [pltpu.VMEM((3 * PT, JW * M), BF)] * 2


def local(modes, weights, counts, mode_index):
    odd = lax.rem(lax.axis_index("gx"), 2)
    levels = jnp.arange(LV, dtype=jnp.int32)
    wt = jnp.swapaxes(weights, 1, 2)
    sw = jnp.where(levels[None, None, :] < counts[0], wt, jnp.zeros_like(wt))
    flat = modes.reshape(3, 2, ROWS, M)

    count_z = lax.axis_size("gz")
    up = [(i, (i + 1) % count_z) for i in range(count_z)]
    down = [(t, s) for s, t in up]
    zlo = lax.ppermute(modes[:, :, :, CZ - 1, :], "gz", up)
    zhi = lax.ppermute(modes[:, :, :, 0, :], "gz", down)
    count_x = lax.axis_size("gx")
    inside = [(i, i ^ 1) for i in range(count_x)]
    across = [(i, (i + 1) % count_x if i % 2 else (i - 1) % count_x) for i in range(count_x)]
    near = lax.ppermute(lax.dynamic_index_in_dim(flat, 1 - odd, 1, keepdims=False), "gx", inside)
    zero = jnp.zeros((), odd.dtype)
    sent = lax.dynamic_slice(flat, (zero, odd, HALF * (1 - odd), zero), (3, 1, HALF, M))
    swsent = lax.dynamic_slice(sw, (odd, zero, (LV // 2) * (1 - odd)), (1, CZ, LV // 2))[0]
    far = lax.ppermute(sent.reshape(3, HALF, M), "gx", across)
    swfar = lax.ppermute(swsent, "gx", across)

    total = pl.pallas_call(
        local_kernel,
        out_shape=jax.ShapeDtypeStruct((M, JW * M), F32),
        in_specs=[HB, VM, VM, VM, VM, SM],
        out_specs=VM,
        scratch_shapes=[
            pltpu.VMEM((3, 2, ROWS + 2 * PAD, M), BF),
            pltpu.VMEM((9, PT, M), F32),
            pltpu.VMEM((PT, M), F32),
            pltpu.VMEM((2 * CH, 2 * CH), BF),
            pltpu.VMEM((3 * M, M), BF),
            *buffers(),
            pltpu.SemaphoreType.DMA((6,)),
        ],
        compiler_params=pltpu.CompilerParams(vmem_limit_bytes=32 << 20),
        cost_estimate=pl.CostEstimate(flops=6 << 30, bytes_accessed=4 << 20, transcendentals=0),
    )(flat, near, zlo, zhi, sw, mode_index)

    start = HALF * odd
    mine = lax.dynamic_slice(flat, (zero, odd, start, zero), (3, 1, HALF, M)).reshape(3, HALF, M)
    swmine = lax.dynamic_slice(sw, (odd, zero, (LV // 2) * odd), (1, CZ, LV // 2))[0]
    part = pl.pallas_call(
        cross_kernel,
        out_shape=jax.ShapeDtypeStruct((16, 8, JW * M), F32),
        in_specs=[VM, VM, VM, VM, VM, SM],
        out_specs=VM,
        scratch_shapes=[
            pltpu.VMEM((M, JW * M), F32),
            pltpu.VMEM((3, PT, M), F32),
            pltpu.VMEM((PT, M), F32),
            pltpu.VMEM((M, M), BF),
            pltpu.VMEM((M, M), BF),
            *buffers(),
        ],
        compiler_params=pltpu.CompilerParams(vmem_limit_bytes=32 << 20),
        cost_estimate=pl.CostEstimate(flops=2 << 30, bytes_accessed=4 << 20, transcendentals=0),
    )(total, mine, far, swmine, swfar, mode_index)

    return pl.pallas_call(
        reduce_kernel,
        out_shape=jax.ShapeDtypeStruct((JW, 4, M), F32),
        in_specs=[VM],
        out_specs=VM,
        scratch_shapes=[
            pltpu.VMEM((16, 8, 8 * M), F32),
            pltpu.VMEM((16, 8, 8 * M), BF),
            pltpu.VMEM((16, 8, 8 * M), BF),
            pltpu.VMEM((2, 4, 8 * M), F32),
            pltpu.VMEM((8, 4, 8 * M), F32),
            pltpu.VMEM((JW, 4, M), F32),
            pltpu.SemaphoreType.DMA((4,)),
            pltpu.SemaphoreType.DMA((4,)),
            pltpu.SemaphoreType.DMA((16,)),
            pltpu.SemaphoreType.DMA((16,)),
            pltpu.SemaphoreType.DMA((8,)),
            pltpu.SemaphoreType.DMA((8,)),
            pltpu.SemaphoreType.DMA((2,)),
        ],
        compiler_params=pltpu.CompilerParams(collective_id=0, has_side_effects=True),
    )(part)


def solution(mesh):
    placed = (P(None, "gx", None, "gz", None), P("gx", None, "gz"), P(("gx", "gz")), P())
    return jax.shard_map(
        local, mesh=mesh, in_specs=placed, out_specs=P(None, "gz", None), check_vma=False
    )
```

time: 249 us -> 88.9 us (0.36); the launches traced: 246 us -> 88.7 us
  matrix products: 84.1 us -> 0 us
  Pallas kernels: 0 us -> 64.8 us
  local copies, waits for them, and re-layouts: 61.1 us -> 7.44 us
  blocking collectives: 41.4 us -> 0 us
  waiting for transfers between devices: 29.4 us -> 3.98 us
  other arithmetic: 17.6 us -> 0.01 us
    dot_general x48 -> x0, matrix products: 84.1 us -> none  [the longest x16 65.3 us: add_block(): jnp.einsum('dqj,dcqk->jcqk', picked, gradient, precision=highest)]
    pallas_call x0 -> x3, Pallas kernels: none -> 64.8 us  [the longest x1 29.7 us: local(): pl.pallas_call(local_kernel, out_shape=jax.ShapeDtypeStruct((M, JW * M),...]
    all_to_all x2 -> x0, blocking collectives: 41.4 us -> none  [the longest x1 20.9 us: sent_to_all(): lax.all_to_all(jnp.broadcast_to(value[None], (count, *value.shape)), axis...]
    slice x18 -> x1, local copies, waits for them, and re-layouts: 31.5 us -> 0.59 us  [local(): zhi = lax.ppermute(modes[:, :, :, 0, :], 'gz', down)]
    ppermute x4 -> x5, waiting for transfers between devices: 29.4 us -> 3.98 us  [the longest x1 3.9 us: local(): zhi = lax.ppermute(modes[:, :, :, 0, :], 'gz', down)]
    another operation x48 -> x0, local copies, waits for them, and re-layouts: 20.5 us -> none  [add_block(): gradient = jnp.stack([grad_x, grad_y, grad_z]).reshape(3, 3, points, size_m)]
    lt x16 -> x1, other arithmetic: 10.5 us -> 0.01 us  [local(): sw = jnp.where(levels[None, None, :] < counts[0], wt, jnp.zeros_like(wt))]
    concatenate x1 -> x0, other arithmetic: 4.49 us -> none  [padded_2(): block = jnp.concatenate([low, block, high], axis=dim)]
  transfers between devices with their start and end apart: 4 -> 5, of which waited for: 3 -> 2; matrix products, arithmetic and copies ran while one was open for 0% -> 3% of each run, Pallas kernels for 0% -> 34%
where the time goes in v1:
time: 88.9 us; the launch traced here: 88.7 us
  Pallas kernels  64.8 us (73%)
  starting transfers between devices  11.7 us (13%)
  local copies, waits for them, and re-layouts  7.44 us (8%)
  waiting for transfers between devices  3.98 us (4%)
    pallas_call x1, Pallas kernels, local(): pl.pallas_call(local_kernel, out_shape=jax.ShapeDtypeStruct((M, JW * M),...  29.7 us
    pallas_call x1, Pallas kernels, local(): pl.pallas_call(reduce_kernel, out_shape=jax.ShapeDtypeStruct((JW, 4, M),...  24.4 us
    pallas_call x1, Pallas kernels, local(): pl.pallas_call(cross_kernel, out_shape=jax.ShapeDtypeStruct((16, 8, JW *...  10.6 us
    ppermute x1, starting transfers between devices, local(): zhi = lax.ppermute(modes[:, :, :, 0, :], 'gz', down)  5.68 us
    ppermute x1, waiting for transfers between devices, local(): zhi = lax.ppermute(modes[:, :, :, 0, :], 'gz', down)  3.9 us
    unnamed x11, local copies, waits for them, and re-layouts  3.77 us
    ppermute x1, starting transfers between devices, local(): lax.ppermute(lax.dynamic_index_in_dim(flat, 1 - odd, 1, keepdims=False),...  3.2 us
    squeeze x1, local copies, waits for them, and re-layouts, local(): lax.dynamic_index_in_dim(flat, 1 - odd, 1, keepdims=False)  2.19 us
  transfers between devices with their start and end apart: 5, of which 2 were waited for; matrix products, arithmetic and copies ran while one was open for 3% of the time, Pallas kernels for 34%

profile of v1, /device:TPU:1, one launch (start us, length us, event | category | flops | bytes accessed | tf_op | source)
XLA Modules:
  0.0 88.7 jit_solution(17455446055295550511)
XLA Ops:
  0.0 0.0 copy-start
  0.0 2.2 %dynamic-slice_bitcast_fusion = bf16[3,1024,128]{2,1,0:T(8,128)(2,1)} fusion(bf16[3,2,1024,128]{3,2,1,0:T(8,128)(2,1)} %bitcast.25, s32[]{:T(128)S(6)} %select_n.28), kind=kLoop, calls=%fused_computation | loop fusion | bytes 1572868 | tf_op jit(solution)/shard_map/jit(dynamic_index_in_dim)/squeeze | solution.py:310
  2.2 3.2 %collective-permute-start = (bf16[3,1024,128]{2,1,0:T(8,128)(2,1)}, bf16[3,1024,128]{2,1,0:T(8,128)(2,1)S(1)}, u32[]{:S(2)}, u32[]{:S(2)}) collective-permute-start(bf16[3,1024,128]{2,1,0:T(8,128)(2,1)} %dynamic-slice_bitcast_fusion), channel_id=1, source_target_pairs={{0,32},{32,0},{64,96},{96,64},{128,160},{160,128},{192,224},{224,1... | collective-permute-start | bytes 2359304 | tf_op jit(solution)/shard_map/ppermute | solution.py:310
  5.4 0.0 copy-done
  5.4 0.6 fusion
  6.0 0.0 copy-start.3
  6.0 0.0 copy-start.2
  6.0 0.7 copy.12
  6.7 0.0 collective-permute-start.1
  6.7 0.7 copy.11
  7.4 5.7 %collective-permute-start.2 = (bf16[3,2,128,128]{3,2,1,0:T(8,128)(2,1)}, bf16[3,2,128,128]{3,2,1,0:T(8,128)(2,1)S(1)}, u32[]{:S(2)}, u32[]{:S(2)}) collective-permute-start(bf16[3,2,128,128]{3,2,1,0:T(8,128)(2,1)} %bitcast.22), channel_id=1, source_target_pairs={{1,0},{2,1},{3,2},{4,3},{5,4},{6,5},{7,6},{8,7},{9,8},{10,9},{11,1... | collective-permute-start | bytes 589832 | tf_op jit(solution)/shard_map/ppermute | solution.py:306
  13.1 0.8 dynamic-slice_bitcast_fusion.1
  13.9 2.1 %collective-permute-start.3 = (bf16[3,512,128]{2,1,0:T(8,128)(2,1)}, bf16[3,512,128]{2,1,0:T(8,128)(2,1)S(1)}, u32[]{:S(2)}, u32[]{:S(2)}) collective-permute-start(bf16[3,512,128]{2,1,0:T(8,128)(2,1)} %get-tuple-element.5), channel_id=1, source_target_pairs={{0,224},{32,64},{64,32},{96,128},{128,96},{160,192},{192,160},{224... | collective-permute-start | bytes 1179656 | tf_op jit(solution)/shard_map/ppermute | solution.py:314
  16.6 0.0 copy-done.3
  16.7 0.1 dynamic-slice_bitcast_fusion.3
  16.8 0.8 collective-permute-start.4
  17.6 0.1 collective-permute-done.1.zlo
  17.6 3.9 %collective-permute-done.2.zhi = bf16[3,2,128,128]{3,2,1,0:T(8,128)(2,1)S(1)} collective-permute-done((bf16[3,2,128,128]{3,2,1,0:T(8,128)(2,1)}, bf16[3,2,128,128]{3,2,1,0:T(8,128)(2,1)S(1)}, u32[]{:S(2)}, u32[]{:S(2)}) %collective-permute-start.2) | collective-permute-done | bytes 196640 | tf_op jit(solution)/shard_map/ppermute | solution.py:306
  21.5 0.0 collective-permute-done.near
  21.5 0.0 copy-done.2
  21.5 29.7 %shard_map.46.total_in = f32[128,2048]{1,0:T(8,128)S(1)} custom-call(bf16[3,2,1024,128]{3,2,1,0:T(8,128)(2,1)S(1)} %bitcast.27, bf16[3,1024,128]{2,1,0:T(8,128)(2,1)S(1)} %collective-permute-done.near, bf16[3,2,128,128]{3,2,1,0:T(8,128)(2,1)S(1)} %collective-permute-done.1.zlo, bf16[3,2,128,128]{3,2,1,0:T(8,128)(2,1)S(1)} %collective-permute-done.2.zhi, ...), custom_call_target="tpu_custom_call" | custom-call | flops 6442450944 | bytes 4194304 | tf_op jit(solution)/shard_map/pallas_call | solution.py:317
  51.3 0.0 collective-permute-done.4.swfar
  51.3 0.0 collective-permute-done.3.far
  51.3 10.6 %shard_map.47.part = f32[16,8,2048]{2,1,0:T(8,128)S(1)} custom-call(f32[128,2048]{1,0:T(8,128)S(1)} %shard_map.46.total_in, bf16[3,512,128]{2,1,0:T(8,128)(2,1)S(1)} %get-tuple-element.6.mine, bf16[3,512,128]{2,1,0:T(8,128)(2,1)S(1)} %collective-permute-done.3.far, f32[8,64]{1,0:T(8,128)S(1)} %get-tuple-element.10.sw, ...), custom_call_target="tpu_custom_call" | custom-call | flops 2147483648 | bytes 4194304 | tf_op jit(solution)/shard_map/pallas_call | solution.py:338
  61.9 0.0 copy-start.1
  61.9 1.0 %copy-done.1 = f32[16,8,2048]{2,1,0:T(8,128)} copy-done((f32[16,8,2048]{2,1,0:T(8,128)}, f32[16,8,2048]{2,1,0:T(8,128)S(1)}, u32[]{:S(2)}) %copy-start.1) | copy-done | bytes 1048600
  62.9 24.4 %shard_map.48 = f32[16,4,128]{2,1,0:T(4,128)} custom-call(f32[16,8,2048]{2,1,0:T(8,128)} %copy-done.1), custom_call_target="tpu_custom_call" | custom-call | tf_op jit(solution)/shard_map/pallas_call | solution.py:355
  87.3 1.4 %copy.15 = f32[16,4,128]{2,1,0:T(4,128)} copy(f32[16,4,128]{2,1,0:T(4,128)} %shard_map.48) | data formatting | bytes 65536
  (3 shorter events, 0.0 us)
Async XLA Ops:
  0.0 5.4 %copy-start = (bf16[3,2,128,8,128]{4,3,2,1,0:T(8,128)(2,1)S(1)}, bf16[3,2,128,8,128]{4,3,2,1,0:T(8,128)(2,1)}, u32[]{:S(2)}) copy-start(bf16[3,2,128,8,128]{4,3,2,1,0:T(8,128)(2,1)} %param.4) | copy-start | bytes 4718596
  2.2 19.3 %collective-permute-start = (bf16[3,1024,128]{2,1,0:T(8,128)(2,1)}, bf16[3,1024,128]{2,1,0:T(8,128)(2,1)S(1)}, u32[]{:S(2)}, u32[]{:S(2)}) collective-permute-start(bf16[3,1024,128]{2,1,0:T(8,128)(2,1)} %dynamic-slice_bitcast_fusion), channel_id=1, source_target_pairs={{0,32},{32,0},{64,96},{96,64},{128,160},{160,128},{192,224},{224,1... | collective-permute-start | bytes 2359304 | tf_op jit(solution)/shard_map/ppermute | solution.py:310
  6.0 10.7 %copy-start.3 = (f32[2,128,8]{1,2,0:T(8,128)S(1)}, f32[2,128,8]{1,2,0:T(8,128)}, u32[]{:S(2)}) copy-start(f32[2,128,8]{1,2,0:T(8,128)} %param.5) | copy-start | bytes 24580
  6.0 15.5 %copy-start.2 = (s32[16]{0:T(128)S(1)}, s32[16]{0:T(128)}, u32[]{:S(2)}) copy-start(s32[16]{0:T(128)} %idx.3) | copy-start | bytes 196
  6.7 10.9 %collective-permute-start.1 = (bf16[3,2,128,128]{3,2,1,0:T(8,128)(2,1)}, bf16[3,2,128,128]{3,2,1,0:T(8,128)(2,1)S(1)}, u32[]{:S(2)}, u32[]{:S(2)}) collective-permute-start(bf16[3,2,128,128]{3,2,1,0:T(8,128)(2,1)} %bitcast.23), channel_id=1, source_target_pairs={{0,1},{1,2},{2,3},{3,4},{4,5},{5,6},{6,7},{7,8},{8,9},{9,10},{10,1... | collective-permute-start | bytes 589832 | tf_op jit(solution)/shard_map/ppermute | solution.py:305
  7.4 14.1 %collective-permute-start.2 = (bf16[3,2,128,128]{3,2,1,0:T(8,128)(2,1)}, bf16[3,2,128,128]{3,2,1,0:T(8,128)(2,1)S(1)}, u32[]{:S(2)}, u32[]{:S(2)}) collective-permute-start(bf16[3,2,128,128]{3,2,1,0:T(8,128)(2,1)} %bitcast.22), channel_id=1, source_target_pairs={{1,0},{2,1},{3,2},{4,3},{5,4},{6,5},{7,6},{8,7},{9,8},{10,9},{11,1... | collective-permute-start | bytes 589832 | tf_op jit(solution)/shard_map/ppermute | solution.py:306
  13.9 37.3 %collective-permute-start.3 = (bf16[3,512,128]{2,1,0:T(8,128)(2,1)}, bf16[3,512,128]{2,1,0:T(8,128)(2,1)S(1)}, u32[]{:S(2)}, u32[]{:S(2)}) collective-permute-start(bf16[3,512,128]{2,1,0:T(8,128)(2,1)} %get-tuple-element.5), channel_id=1, source_target_pairs={{0,224},{32,64},{64,32},{96,128},{128,96},{160,192},{192,160},{224... | collective-permute-start | bytes 1179656 | tf_op jit(solution)/shard_map/ppermute | solution.py:314
  16.8 34.5 %collective-permute-start.4 = (f32[8,64]{1,0:T(8,128)S(1)}, f32[8,64]{1,0:T(8,128)S(1)}, u32[]{:S(2)}, u32[]{:S(2)}) collective-permute-start(f32[8,64]{1,0:T(8,128)S(1)} %get-tuple-element.9), channel_id=1, source_target_pairs={{0,224},{32,64},{64,32},{96,128},{128,96},{160,192},{192,160},{224... | collective-permute-start | bytes 6152 | tf_op jit(solution)/shard_map/ppermute | solution.py:315
  61.9 1.0 %copy-start.1 = (f32[16,8,2048]{2,1,0:T(8,128)}, f32[16,8,2048]{2,1,0:T(8,128)S(1)}, u32[]{:S(2)}) copy-start(f32[16,8,2048]{2,1,0:T(8,128)S(1)} %shard_map.47.part) | copy-start | bytes 3145732

commit v2 on v1

--- a/solution.py
+++ b/solution.py
@@ -18,8 +18,6 @@
 PAD = 16
 CH = 128
 PT = 2 * CH
-GRP = 32
-STEPS = PT // GRP
 HALF = ROWS // 2
 
 
@@ -27,44 +25,60 @@
     return lax.broadcasted_iota(jnp.int32, shape, dim)
 
 
-def pick_matrix(idx_ref, scales):
-    lane = iota((1, M), 1)
-    wanted = jnp.zeros((1, M), jnp.int32)
+def pick_rows(idx_ref, scales):
+    count = len(scales) * JW
+    row, col = iota((count, M), 0), iota((count, M), 1)
+    wanted = jnp.zeros((count, M), jnp.int32)
     for j in range(JW):
-        wanted = jnp.where(lane % JW == j, idx_ref[j], wanted)
-    wanted = jnp.broadcast_to(wanted, (M, M))
-    row, col = iota((M, M), 0), iota((M, M), 1)
-    blocks = []
-    for d, scale in enumerate(scales):
-        hit = (row == wanted) & (col // JW == d)
-        blocks.append(jnp.where(hit, scale, 0.0).astype(BF))
-    return blocks
-
-
-def weighted_columns(sw, first):
+        wanted = jnp.where(row % JW == j, idx_ref[j], wanted)
+    blocks = [
+        jnp.where((col == wanted) & (row // JW == d), scale, 0.0).astype(BF)
+        for d, scale in enumerate(scales)
+    ]
+    return jnp.concatenate(blocks, axis=1)
+
+
+def weighted_columns(sw, first, levels):
     return jnp.concatenate(
-        [jnp.broadcast_to(sw[:, y : y + 1], (CZ, M)) for y in range(first, first + CH // CZ)], axis=0
+        [jnp.broadcast_to(sw[:, y : y + 1], (CZ, M)) for y in range(first, first + levels)], axis=0
     )
 
 
-def dot_part(total, tested, spread, step):
-    cols = pl.ds(pl.multiple_of(step * 256, 256), 256)
-    total[:, cols] += jnp.dot(tested[...], spread[:, cols], preferred_element_type=F32)
+def stencil_matrix():
+    row, col = iota((PT, PT), 0), iota((PT, PT), 1)
+    point = lax.rem(col, CH)
+    lev, z = point // CZ, lax.rem(point, CZ)
+    up = jnp.where(point + CZ < CH, point + CZ, point + CZ + 16)
+    down = jnp.where(point >= CZ, point - CZ, CH + 8 + point)
+    ahead = jnp.where(z < CZ - 1, point + 1, CH + 48 + lev)
+    behind = jnp.where(z > 0, point - 1, CH + 32 + lev)
+    plus = jnp.where(col < CH, up, ahead)
+    minus = jnp.where(col < CH, down, behind)
+    return (jnp.where(row == plus, 1.0, 0.0) - jnp.where(row == minus, 1.0, 0.0)).astype(BF)
 
 
 def run_chunks(total, tested, spread, prepare, terms, count):
-    for k in range(count + 1):
-        if k < count:
-            prepare(k, tested[k % 2])
-
-        def step(s, carry, k=k):
-            if k > 0:
-                dot_part(total, tested[(k - 1) % 2], spread[(k - 1) % 2], s)
-            if k < count:
-                terms(s, spread[k % 2])
+    def dot(step, buffer, k):
+        rows = pl.ds(pl.multiple_of(step * 256, 256), 256)
+        total[rows, :] += jnp.dot(spread[buffer][...], tested[k % 2][...], preferred_element_type=F32)
+
+    for k in range(count):
+        prepare(k)
+        if k > 0:
+            dot(7, 1, k - 1)
+        terms(k, 0, spread[0])
+
+        def body(m, carry, k=k):
+            dot(2 * m, 0, k)
+            terms(k, 2 * m + 1, spread[1])
+            dot(2 * m + 1, 1, k)
+            terms(k, 2 * m + 2, spread[0])
             return carry
 
-        lax.fori_loop(0, STEPS, step, 0)
+        lax.fori_loop(0, 3, body, 0)
+        dot(6, 0, k)
+        terms(k, 7, spread[1])
+    dot(7, 1, count - 1)
 
 
 def local_kernel(
@@ -86,58 +100,61 @@
         for side in range(2):
             planes[c, side, pl.ds(0, PAD), :] = jnp.zeros((PAD, M), BF)
             planes[c, side, pl.ds(PAD + ROWS, PAD), :] = jnp.zeros((PAD, M), BF)
-    row, col = iota((2 * CH, 2 * CH), 0), iota((2 * CH, 2 * CH), 1)
-    point = lax.rem(row, CH)
-    lev, z = point // CZ, lax.rem(point, CZ)
-    here = point + PAD
-    in_y = jnp.where(col == here + CZ, 1.0, 0.0) - jnp.where(col == here - CZ, 1.0, 0.0)
-    ahead = jnp.where(z < CZ - 1, here + 1, 2 * PAD + CH + 16 + lev)
-    behind = jnp.where(z > 0, here - 1, 2 * PAD + CH + lev)
-    in_z = jnp.where(col == ahead, 1.0, 0.0) - jnp.where(col == behind, 1.0, 0.0)
-    stencil[...] = jnp.where(row < CH, in_y, in_z).astype(BF)
-    for d, block in enumerate(pick_matrix(idx, (sign, 0.5, 0.5))):
-        sel[d * M : (d + 1) * M, :] = block
+    stencil[...] = stencil_matrix()
+    sel[...] = pick_rows(idx, (sign, 0.5, 0.5))
     total[...] = jnp.zeros_like(total)
     for copy in copies:
         copy.wait()
 
-    def prepare(k, tested):
-        first = k * CH
+    def prepare(k):
+        first = PAD + k * CH
+        g, b = grad[k % 2], k % 2
+        turned = [[], []]
         for side in range(2):
             which = odd if side == 0 else 1 - odd
-            wide = weighted_columns(sw[which], k * (CH // CZ))
-            rows = slice(side * CH, (side + 1) * CH)
-            mine = []
+            wide = weighted_columns(sw[which], k * (CH // CZ), CH // CZ)
+            lanes = slice(side * CH, (side + 1) * CH)
             for c in range(3):
-                window = planes[c, side, first : first + CH + 2 * PAD, :]
-                lo = zlo[c, which, k * 16 : (k + 1) * 16, :]
-                hi = zhi[c, which, k * 16 : (k + 1) * 16, :]
-                stacked = jnp.concatenate([window, lo, hi, jnp.zeros((64, M), BF)], axis=0)
-                both = jnp.dot(stencil[...], stacked, preferred_element_type=F32)
-                grad[3 + c, rows, :] = both[:CH]
-                grad[6 + c, rows, :] = both[CH:]
-                here = window[PAD : PAD + CH]
-                mine.append(here)
-                here = here.astype(F32)
-                other = planes[c, 1 - side, PAD + first : PAD + first + CH, :].astype(F32)
-                if side == 0:
-                    grad[c, rows, :] = other
-                else:
-                    grad[c, rows, :] = near[c, first : first + CH, :].astype(F32) - other
+                here = planes[c, side, first : first + CH, :]
+                stacked = jnp.concatenate(
+                    [
+                        here,
+                        planes[c, side, first - 16 : first, :],
+                        planes[c, side, first + CH : first + CH + 16, :],
+                        zlo[c, which, k * 16 : (k + 1) * 16, :],
+                        zhi[c, which, k * 16 : (k + 1) * 16, :],
+                        jnp.zeros((64, M), BF),
+                    ],
+                    axis=0,
+                ).T
+                both = jnp.dot(stacked, stencil[...], preferred_element_type=F32)
+                g[3 + c, :, lanes] = both[:, :CH]
+                g[6 + c, :, lanes] = both[:, CH:]
+                turned[side].append(stacked[:, :CH])
                 at = c * PT + side * CH
-                tested[:, at : at + CH] = (here * wide).T.astype(BF)
-            picks[rows, :] = jnp.dot(jnp.concatenate(mine, axis=1), sel[...], preferred_element_type=F32)
-
-    def terms(s, spread):
-        rows = pl.ds(pl.multiple_of(s * GRP, GRP), GRP)
-        pk = picks[rows, :]
-        g = [grad[q, rows, :] for q in range(9)]
-        for j in range(JW):
-            px, py, pz = [jnp.broadcast_to(pk[:, d * JW + j : d * JW + j + 1], (GRP, M)) for d in range(3)]
-            for c in range(3):
-                value = px * g[c] + py * g[3 + c] + pz * g[6 + c]
-                at = pl.ds(pl.multiple_of(c * PT + s * GRP, GRP), GRP)
-                spread[at, j * M : (j + 1) * M] = value.astype(BF)
+                (tt0, tt1)[b][at : at + CH, :] = (here.astype(F32) * wide).astype(BF)
+            pk = jnp.dot(sel[...], jnp.concatenate(turned[side], axis=0), preferred_element_type=F32)
+            for r in range(3 * JW):
+                picks[b][r, :, lanes] = jnp.broadcast_to(pk[r : r + 1], (8, CH))
+        for c in range(3):
+            g[c, :, :CH] = turned[1][c].astype(F32)
+            beyond = near[c, k * CH : (k + 1) * CH, :].T
+            g[c, :, CH:] = beyond.astype(F32) - turned[0][c].astype(F32)
+
+    def terms(k, step, spread):
+        g, pk = grad[k % 2], picks[k % 2]
+        scale = []
+        for h in range(2):
+            p = [pk[d * JW + 2 * step + h] for d in range(3)]
+            scale.append([jnp.concatenate([v, v], axis=0) for v in p])
+        for c in range(3):
+            for t in range(8):
+                tile = slice(t * 16, t * 16 + 16)
+                gx, gy, gz = g[c, tile, :], g[3 + c, tile, :], g[6 + c, tile, :]
+                for h in range(2):
+                    px, py, pz = scale[h]
+                    value = px * gx + py * gy + pz * gz
+                    spread[h * M + t * 16 : h * M + t * 16 + 16, c * PT : (c + 1) * PT] = value.astype(BF)
 
     run_chunks(total, (tt0, tt1), (sp0, sp1), prepare, terms, ROWS // CH)
 
@@ -147,39 +164,40 @@
 ):
     odd = lax.rem(lax.axis_index("gx"), 2)
     sign = jnp.where(odd == 0, 0.5, -0.5).astype(F32)
-    selp[...] = pick_matrix(idx, (sign,))[0]
-    seln[...] = pick_matrix(idx, (-sign,))[0]
+    selp[...] = pick_rows(idx, (sign,))
+    seln[...] = pick_rows(idx, (-sign,))
     total[...] = total_in[...]
 
-    def prepare(k, tested):
-        first = (k % 2) * PT
+    def prepare(k):
+        first, b = (k % 2) * PT, k % 2
         own = k < 2
         tsrc, vsrc, w, sel = (mine, far, sw, seln) if own else (far, mine, swfar, selp)
-        wide = jnp.concatenate(
-            [weighted_columns(w[...], (k % 2) * 32), weighted_columns(w[...], (k % 2) * 32 + 16)], axis=0
-        )
+        wide = weighted_columns(w[...], (k % 2) * 32, 32)
         for c in range(3):
             here = tsrc[c, first : first + PT, :]
             if c == 0:
-                picks[...] = jnp.dot(here, sel[...], preferred_element_type=F32)
-            tested[:, c * PT : (c + 1) * PT] = (here.astype(F32) * wide).T.astype(BF)
-            vals[c] = vsrc[c, first : first + PT, :].astype(F32)
-
-    def terms(s, spread):
-        rows = pl.ds(pl.multiple_of(s * GRP, GRP), GRP)
-        pk = picks[rows, :]
-        v = [vals[c, rows, :] for c in range(3)]
-        for j in range(JW):
-            px = jnp.broadcast_to(pk[:, j : j + 1], (GRP, M))
-            for c in range(3):
-                at = pl.ds(pl.multiple_of(c * PT + s * GRP, GRP), GRP)
-                spread[at, j * M : (j + 1) * M] = (px * v[c]).astype(BF)
+                pk = jnp.dot(sel[...], here.T, preferred_element_type=F32)
+                for j in range(JW):
+                    picks[b][j] = jnp.broadcast_to(pk[j : j + 1], (16, PT)).astype(BF)
+            (tt0, tt1)[b][c * PT : (c + 1) * PT, :] = (here.astype(F32) * wide).astype(BF)
+            vals[b][c] = vsrc[c, first : first + PT, :].T
+
+    def terms(k, step, spread):
+        v, pk = vals[k % 2], picks[k % 2]
+        scale = [pk[2 * step + h] for h in range(2)]
+        for c in range(3):
+            for t in range(8):
+                tile = v[c, t * 16 : t * 16 + 16, :]
+                for h in range(2):
+                    spread[h * M + t * 16 : h * M + t * 16 + 16, c * PT : (c + 1) * PT] = scale[h] * tile
 
     run_chunks(total, (tt0, tt1), (sp0, sp1), prepare, terms, 4)
-    for q in range(16):
-        for low in range(2):
-            owner = (q // 4) * 8 + low * 4 + q % 4
-            out[q, low * 4 : low * 4 + 4, :] = total[owner * 4 : owner * 4 + 4, :]
+    for j in range(JW):
+        block = total[j * M : (j + 1) * M, :].T
+        for q in range(16):
+            for low in range(2):
+                owner = (q // 4) * 8 + low * 4 + q % 4
+                out[q, low * 4 : low * 4 + 4, j * M : (j + 1) * M] = block[owner * 4 : owner * 4 + 4]
 
 
 def reduce_kernel(part, out, pair, send, got, column, stack, whole, asend, arecv, bsend, brecv, csend, crecv, dsem):
@@ -289,7 +307,7 @@
 
 
 def buffers():
-    return [pltpu.VMEM((M, 3 * PT), BF)] * 2 + [pltpu.VMEM((3 * PT, JW * M), BF)] * 2
+    return [pltpu.VMEM((3 * PT, M), BF)] * 2 + [pltpu.VMEM((2 * M, 3 * PT), BF)] * 2
 
 
 def local(modes, weights, counts, mode_index):
@@ -316,15 +334,15 @@
 
     total = pl.pallas_call(
         local_kernel,
-        out_shape=jax.ShapeDtypeStruct((M, JW * M), F32),
+        out_shape=jax.ShapeDtypeStruct((JW * M, M), F32),
         in_specs=[HB, VM, VM, VM, VM, SM],
         out_specs=VM,
         scratch_shapes=[
             pltpu.VMEM((3, 2, ROWS + 2 * PAD, M), BF),
-            pltpu.VMEM((9, PT, M), F32),
-            pltpu.VMEM((PT, M), F32),
-            pltpu.VMEM((2 * CH, 2 * CH), BF),
-            pltpu.VMEM((3 * M, M), BF),
+            [pltpu.VMEM((9, M, PT), F32)] * 2,
+            [pltpu.VMEM((3 * JW, 8, PT), F32)] * 2,
+            pltpu.VMEM((PT, PT), BF),
+            pltpu.VMEM((3 * JW, 3 * M), BF),
             *buffers(),
             pltpu.SemaphoreType.DMA((6,)),
         ],
@@ -341,11 +359,11 @@
         in_specs=[VM, VM, VM, VM, VM, SM],
         out_specs=VM,
         scratch_shapes=[
-            pltpu.VMEM((M, JW * M), F32),
-            pltpu.VMEM((3, PT, M), F32),
-            pltpu.VMEM((PT, M), F32),
-            pltpu.VMEM((M, M), BF),
-            pltpu.VMEM((M, M), BF),
+            pltpu.VMEM((JW * M, M), F32),
+            [pltpu.VMEM((3, M, PT), BF)] * 2,
+            [pltpu.VMEM((JW, 16, PT), BF)] * 2,
+            pltpu.VMEM((JW, M), BF),
+            pltpu.VMEM((JW, M), BF),
             *buffers(),
         ],
         compiler_params=pltpu.CompilerParams(vmem_limit_bytes=32 << 20),

time: 88.9 us -> 74.1 us (0.83)
  Pallas kernels: 64.8 us -> 50 us
    pallas_call x1, Pallas kernels: 29.7 us -> 18.7 us  [local(): pl.pallas_call(local_kernel, out_shape=jax.ShapeDtypeStruct((JW * M, M),...]
    pallas_call x1, Pallas kernels: 10.6 us -> 6.77 us  [local(): pl.pallas_call(cross_kernel, out_shape=jax.ShapeDtypeStruct((16, 8, JW *...]
  transfers between devices with their start and end apart: 5 -> 5, of which waited for: 2 -> 2; matrix products, arithmetic and copies ran while one was open for 3% -> 4% of each run, Pallas kernels for 34% -> 25%
where the time goes in v2:
time: 74.1 us; the launch traced here: 73.9 us
  Pallas kernels  50 us (67%)
  starting transfers between devices  11.7 us (16%)
  local copies, waits for them, and re-layouts  7.44 us (10%)
  waiting for transfers between devices  3.98 us (5%)
  between operations  0.75 us (1%)
    pallas_call x1, Pallas kernels, local(): pl.pallas_call(reduce_kernel, out_shape=jax.ShapeDtypeStruct((JW, 4, M),...  24.4 us
    pallas_call x1, Pallas kernels, local(): pl.pallas_call(local_kernel, out_shape=jax.ShapeDtypeStruct((JW * M, M),...  18.7 us
    pallas_call x1, Pallas kernels, local(): pl.pallas_call(cross_kernel, out_shape=jax.ShapeDtypeStruct((16, 8, JW *...  6.77 us
    ppermute x1, starting transfers between devices, local(): zhi = lax.ppermute(modes[:, :, :, 0, :], 'gz', down)  5.68 us
    ppermute x1, waiting for transfers between devices, local(): zhi = lax.ppermute(modes[:, :, :, 0, :], 'gz', down)  3.9 us
    unnamed x11, local copies, waits for them, and re-layouts  3.77 us
    ppermute x1, starting transfers between devices, local(): lax.ppermute(lax.dynamic_index_in_dim(flat, 1 - odd, 1, keepdims=False),...  3.2 us
    squeeze x1, local copies, waits for them, and re-layouts, local(): lax.dynamic_index_in_dim(flat, 1 - odd, 1, keepdims=False)  2.19 us
  transfers between devices with their start and end apart: 5, of which 2 were waited for; matrix products, arithmetic and copies ran while one was open for 4% of the time, Pallas kernels for 25%

profile of v2, /device:TPU:1, one launch (start us, length us, event | category | flops | bytes accessed | tf_op | source)
XLA Modules:
  0.0 73.9 jit_solution(2998839769367789246)
XLA Ops:
  0.0 0.0 copy-start
  0.0 2.2 %dynamic-slice_bitcast_fusion = bf16[3,1024,128]{2,1,0:T(8,128)(2,1)} fusion(bf16[3,2,1024,128]{3,2,1,0:T(8,128)(2,1)} %bitcast.25, s32[]{:T(128)S(6)} %select_n.28), kind=kLoop, calls=%fused_computation | loop fusion | bytes 1572868 | tf_op jit(solution)/shard_map/jit(dynamic_index_in_dim)/squeeze | solution.py:328
  2.2 3.2 %collective-permute-start = (bf16[3,1024,128]{2,1,0:T(8,128)(2,1)}, bf16[3,1024,128]{2,1,0:T(8,128)(2,1)S(1)}, u32[]{:S(2)}, u32[]{:S(2)}) collective-permute-start(bf16[3,1024,128]{2,1,0:T(8,128)(2,1)} %dynamic-slice_bitcast_fusion), channel_id=1, source_target_pairs={{0,32},{32,0},{64,96},{96,64},{128,160},{160,128},{192,224},{224,1... | collective-permute-start | bytes 2359304 | tf_op jit(solution)/shard_map/ppermute | solution.py:328
  5.4 0.0 copy-done
  5.4 0.6 fusion
  6.0 0.0 copy-start.3
  6.0 0.0 copy-start.2
  6.0 0.7 copy.12
  6.7 0.0 collective-permute-start.1
  6.7 0.7 copy.11
  7.4 5.7 %collective-permute-start.2 = (bf16[3,2,128,128]{3,2,1,0:T(8,128)(2,1)}, bf16[3,2,128,128]{3,2,1,0:T(8,128)(2,1)S(1)}, u32[]{:S(2)}, u32[]{:S(2)}) collective-permute-start(bf16[3,2,128,128]{3,2,1,0:T(8,128)(2,1)} %bitcast.22), channel_id=1, source_target_pairs={{1,0},{2,1},{3,2},{4,3},{5,4},{6,5},{7,6},{8,7},{9,8},{10,9},{11,1... | collective-permute-start | bytes 589832 | tf_op jit(solution)/shard_map/ppermute | solution.py:324
  13.1 0.8 %dynamic-slice_bitcast_fusion.1 = (bf16[3,512,128]{2,1,0:T(8,128)(2,1)}, bf16[3,512,128]{2,1,0:T(8,128)(2,1)S(1)}) fusion(bf16[3,2,1024,128]{3,2,1,0:T(8,128)(2,1)S(1)} %bitcast.26, s32[]{:T(128)S(6)} %select_n.31, s32[]{:T(128)S(6)} %select_n.33, s32[]{:T(128)S(6)} %select_n.32), kind=kLoop, calls=%fused_computation.1 | loop fusion | bytes 1572876 | tf_op jit(solution)/shard_map/reshape | solution.py:332
  13.9 2.1 %collective-permute-start.3 = (bf16[3,512,128]{2,1,0:T(8,128)(2,1)}, bf16[3,512,128]{2,1,0:T(8,128)(2,1)S(1)}, u32[]{:S(2)}, u32[]{:S(2)}) collective-permute-start(bf16[3,512,128]{2,1,0:T(8,128)(2,1)} %get-tuple-element.5), channel_id=1, source_target_pairs={{0,224},{32,64},{64,32},{96,128},{128,96},{160,192},{192,160},{224... | collective-permute-start | bytes 1179656 | tf_op jit(solution)/shard_map/ppermute | solution.py:332
  16.6 0.0 copy-done.3
  16.7 0.1 dynamic-slice_bitcast_fusion.3
  16.8 0.8 %collective-permute-start.4 = (f32[8,64]{1,0:T(8,128)S(1)}, f32[8,64]{1,0:T(8,128)S(1)}, u32[]{:S(2)}, u32[]{:S(2)}) collective-permute-start(f32[8,64]{1,0:T(8,128)S(1)} %get-tuple-element.9), channel_id=1, source_target_pairs={{0,224},{32,64},{64,32},{96,128},{128,96},{160,192},{192,160},{224... | collective-permute-start | bytes 6152 | tf_op jit(solution)/shard_map/ppermute | solution.py:333
  17.6 0.1 collective-permute-done.1.zlo
  17.6 3.9 %collective-permute-done.2.zhi = bf16[3,2,128,128]{3,2,1,0:T(8,128)(2,1)S(1)} collective-permute-done((bf16[3,2,128,128]{3,2,1,0:T(8,128)(2,1)}, bf16[3,2,128,128]{3,2,1,0:T(8,128)(2,1)S(1)}, u32[]{:S(2)}, u32[]{:S(2)}) %collective-permute-start.2) | collective-permute-done | bytes 196640 | tf_op jit(solution)/shard_map/ppermute | solution.py:324
  21.5 0.0 collective-permute-done.near
  21.5 0.0 copy-done.2
  21.5 18.7 %shard_map.46.total_in = f32[2048,128]{1,0:T(8,128)S(1)} custom-call(bf16[3,2,1024,128]{3,2,1,0:T(8,128)(2,1)S(1)} %bitcast.27, bf16[3,1024,128]{2,1,0:T(8,128)(2,1)S(1)} %collective-permute-done.near, bf16[3,2,128,128]{3,2,1,0:T(8,128)(2,1)S(1)} %collective-permute-done.1.zlo, bf16[3,2,128,128]{3,2,1,0:T(8,128)(2,1)S(1)} %collective-permute-done.2.zhi, ...), custom_call_target="tpu_custom_call" | custom-call | flops 6442450944 | bytes 4194304 | tf_op jit(solution)/shard_map/pallas_call | solution.py:335
  40.3 0.0 collective-permute-done.4.swfar
  40.3 0.0 collective-permute-done.3.far
  40.3 6.8 %shard_map.47.part = f32[16,8,2048]{2,1,0:T(8,128)S(1)} custom-call(f32[2048,128]{1,0:T(8,128)S(1)} %shard_map.46.total_in, bf16[3,512,128]{2,1,0:T(8,128)(2,1)S(1)} %get-tuple-element.6.mine, bf16[3,512,128]{2,1,0:T(8,128)(2,1)S(1)} %collective-permute-done.3.far, f32[8,64]{1,0:T(8,128)S(1)} %get-tuple-element.10.sw, ...), custom_call_target="tpu_custom_call" | custom-call | flops 2147483648 | bytes 4194304 | tf_op jit(solution)/shard_map/pallas_call | solution.py:356
  47.1 0.0 copy-start.1
  47.1 1.0 %copy-done.1 = f32[16,8,2048]{2,1,0:T(8,128)} copy-done((f32[16,8,2048]{2,1,0:T(8,128)}, f32[16,8,2048]{2,1,0:T(8,128)S(1)}, u32[]{:S(2)}) %copy-start.1) | copy-done | bytes 1048600
  48.0 24.4 %shard_map.48 = f32[16,4,128]{2,1,0:T(4,128)} custom-call(f32[16,8,2048]{2,1,0:T(8,128)} %copy-done.1), custom_call_target="tpu_custom_call" | custom-call | tf_op jit(solution)/shard_map/pallas_call | solution.py:373
  72.5 1.4 %copy.15 = f32[16,4,128]{2,1,0:T(4,128)} copy(f32[16,4,128]{2,1,0:T(4,128)} %shard_map.48) | data formatting | bytes 65536
  (3 shorter events, 0.0 us)
Async XLA Ops:
  0.0 5.4 %copy-start = (bf16[3,2,128,8,128]{4,3,2,1,0:T(8,128)(2,1)S(1)}, bf16[3,2,128,8,128]{4,3,2,1,0:T(8,128)(2,1)}, u32[]{:S(2)}) copy-start(bf16[3,2,128,8,128]{4,3,2,1,0:T(8,128)(2,1)} %param.4) | copy-start | bytes 4718596
  2.2 19.3 %collective-permute-start = (bf16[3,1024,128]{2,1,0:T(8,128)(2,1)}, bf16[3,1024,128]{2,1,0:T(8,128)(2,1)S(1)}, u32[]{:S(2)}, u32[]{:S(2)}) collective-permute-start(bf16[3,1024,128]{2,1,0:T(8,128)(2,1)} %dynamic-slice_bitcast_fusion), channel_id=1, source_target_pairs={{0,32},{32,0},{64,96},{96,64},{128,160},{160,128},{192,224},{224,1... | collective-permute-start | bytes 2359304 | tf_op jit(solution)/shard_map/ppermute | solution.py:328
  6.0 10.7 %copy-start.3 = (f32[2,128,8]{1,2,0:T(8,128)S(1)}, f32[2,128,8]{1,2,0:T(8,128)}, u32[]{:S(2)}) copy-start(f32[2,128,8]{1,2,0:T(8,128)} %param.5) | copy-start | bytes 24580
  6.0 15.5 %copy-start.2 = (s32[16]{0:T(128)S(1)}, s32[16]{0:T(128)}, u32[]{:S(2)}) copy-start(s32[16]{0:T(128)} %idx.3) | copy-start | bytes 196
  6.7 10.9 %collective-permute-start.1 = (bf16[3,2,128,128]{3,2,1,0:T(8,128)(2,1)}, bf16[3,2,128,128]{3,2,1,0:T(8,128)(2,1)S(1)}, u32[]{:S(2)}, u32[]{:S(2)}) collective-permute-start(bf16[3,2,128,128]{3,2,1,0:T(8,128)(2,1)} %bitcast.23), channel_id=1, source_target_pairs={{0,1},{1,2},{2,3},{3,4},{4,5},{5,6},{6,7},{7,8},{8,9},{9,10},{10,1... | collective-permute-start | bytes 589832 | tf_op jit(solution)/shard_map/ppermute | solution.py:323
  7.4 14.1 %collective-permute-start.2 = (bf16[3,2,128,128]{3,2,1,0:T(8,128)(2,1)}, bf16[3,2,128,128]{3,2,1,0:T(8,128)(2,1)S(1)}, u32[]{:S(2)}, u32[]{:S(2)}) collective-permute-start(bf16[3,2,128,128]{3,2,1,0:T(8,128)(2,1)} %bitcast.22), channel_id=1, source_target_pairs={{1,0},{2,1},{3,2},{4,3},{5,4},{6,5},{7,6},{8,7},{9,8},{10,9},{11,1... | collective-permute-start | bytes 589832 | tf_op jit(solution)/shard_map/ppermute | solution.py:324
  13.9 26.4 %collective-permute-start.3 = (bf16[3,512,128]{2,1,0:T(8,128)(2,1)}, bf16[3,512,128]{2,1,0:T(8,128)(2,1)S(1)}, u32[]{:S(2)}, u32[]{:S(2)}) collective-permute-start(bf16[3,512,128]{2,1,0:T(8,128)(2,1)} %get-tuple-element.5), channel_id=1, source_target_pairs={{0,224},{32,64},{64,32},{96,128},{128,96},{160,192},{192,160},{224... | collective-permute-start | bytes 1179656 | tf_op jit(solution)/shard_map/ppermute | solution.py:332
  16.8 23.5 %collective-permute-start.4 = (f32[8,64]{1,0:T(8,128)S(1)}, f32[8,64]{1,0:T(8,128)S(1)}, u32[]{:S(2)}, u32[]{:S(2)}) collective-permute-start(f32[8,64]{1,0:T(8,128)S(1)} %get-tuple-element.9), channel_id=1, source_target_pairs={{0,224},{32,64},{64,32},{96,128},{128,96},{160,192},{192,160},{224... | collective-permute-start | bytes 6152 | tf_op jit(solution)/shard_map/ppermute | solution.py:333
  47.1 1.0 %copy-start.1 = (f32[16,8,2048]{2,1,0:T(8,128)}, f32[16,8,2048]{2,1,0:T(8,128)S(1)}, u32[]{:S(2)}) copy-start(f32[16,8,2048]{2,1,0:T(8,128)S(1)} %shard_map.47.part) | copy-start | bytes 3145732

commit v3 on v2

v3 whole, which is shorter than its diff:
```python
import functools

import jax
import jax.numpy as jnp
from jax import lax
from jax.experimental import pallas as pl
from jax.experimental.pallas import tpu as pltpu
from jax.sharding import PartitionSpec as P

MESH = pl.DeviceIdType.MESH
BF = jnp.bfloat16
F32 = jnp.float32
M = 128
JW = 16
LV = 128
CZ = 8
ROWS = LV * CZ
PAD = 16
CH = 128
PT = 2 * CH
HALF = ROWS // 2


def iota(shape, dim):
    return lax.broadcasted_iota(jnp.int32, shape, dim)


def pick_rows(idx_ref, scales):
    count = len(scales) * JW
    row, col = iota((count, M), 0), iota((count, M), 1)
    wanted = jnp.zeros((count, M), jnp.int32)
    for j in range(JW):
        wanted = jnp.where(row % JW == j, idx_ref[j], wanted)
    blocks = [
        jnp.where((col == wanted) & (row // JW == d), scale, 0.0).astype(BF)
        for d, scale in enumerate(scales)
    ]
    return jnp.concatenate(blocks, axis=1)


def weighted_columns(sw, first, levels):
    return jnp.concatenate(
        [jnp.broadcast_to(sw[:, y : y + 1], (CZ, M)) for y in range(first, first + levels)], axis=0
    )


def stencil_matrix():
    row, col = iota((PT, PT), 0), iota((PT, PT), 1)
    point = lax.rem(col, CH)
    lev, z = point // CZ, lax.rem(point, CZ)
    up = jnp.where(point + CZ < CH, point + CZ, point + CZ + 16)
    down = jnp.where(point >= CZ, point - CZ, CH + 8 + point)
    ahead = jnp.where(z < CZ - 1, point + 1, CH + 48 + lev)
    behind = jnp.where(z > 0, point - 1, CH + 32 + lev)
    plus = jnp.where(col < CH, up, ahead)
    minus = jnp.where(col < CH, down, behind)
    return (jnp.where(row == plus, 1.0, 0.0) - jnp.where(row == minus, 1.0, 0.0)).astype(BF)


def select_rows():
    row, col = iota((32, CH), 0), iota((32, CH), 1)
    return jnp.where(col == lax.rem(row, 16) * CZ + (row // 16) * (CZ - 1), 1.0, 0.0).astype(BF)


def local_kernel(
    modes, weights, counts, idx, out,
    total, planes, near, far, zsend, zgot, sw, swfar, turned, cross_tested, grads, picks, spread, stencil, sel, self_,
    local_sem, near_s, near_r, far_s, far_r, z_s, z_r, w_sem,
):
    gx, gz = lax.axis_index("gx"), lax.axis_index("gz")
    odd = lax.rem(gx, 2)
    sign = jnp.where(odd == 0, 0.5, -0.5).astype(F32)
    near_peer = (gx + 1 - 2 * odd, gz)
    far_peer = (lax.rem(gx + 7 + 2 * odd, 8), gz)
    z_peers = ((gx, lax.rem(gz + 31, 32)), (gx, lax.rem(gz + 1, 32)))

    copies = []
    for c in range(3):
        for side in range(2):
            which = odd if side == 0 else 1 - odd
            copies.append(
                pltpu.make_async_copy(
                    modes.at[c, which], planes.at[c, side, pl.ds(PAD, ROWS)], local_sem.at[2 * c + side]
                )
            )
            copies[-1].start()
    barrier = pltpu.get_barrier_semaphore()
    for peer in (near_peer, far_peer, *z_peers):
        pl.semaphore_signal(barrier, inc=1, device_id=peer, device_id_type=MESH)
    for c in range(3):
        for side in range(2):
            planes[c, side, pl.ds(0, PAD), :] = jnp.zeros((PAD, M), BF)
            planes[c, side, pl.ds(PAD + ROWS, PAD), :] = jnp.zeros((PAD, M), BF)
    for side in range(2):
        which = odd if side == 0 else 1 - odd
        w = weights[which]
        sw[side] = jnp.where(iota((CZ, LV), 1) < counts[0], w, jnp.zeros_like(w))
    stencil[...] = stencil_matrix()
    sel[...] = pick_rows(idx, (sign, 0.5, 0.5))
    self_[...] = pick_rows(idx, (sign,))
    total[...] = jnp.zeros_like(total)
    spread[1][...] = jnp.zeros_like(spread[1])
    ends = select_rows()
    for copy in copies:
        copy.wait()
    pl.semaphore_wait(barrier, 4)

    def block_of(t):
        return lax.rem(t + 4 * (1 - odd), 8)

    def rows_of(k):
        return pl.ds(pl.multiple_of(PAD + k * CH, 16), CH)

    def near_copy(k):
        return pltpu.make_async_remote_copy(
            src_ref=planes.at[:, 1, rows_of(k)], dst_ref=near.at[k],
            send_sem=near_s.at[k], recv_sem=near_r.at[k], device_id=near_peer, device_id_type=MESH,
        )

    def far_copy(p):
        return pltpu.make_async_remote_copy(
            src_ref=planes.at[:, 0, rows_of(p + 4 * (1 - odd))], dst_ref=far.at[p],
            send_sem=far_s.at[p], recv_sem=far_r.at[p], device_id=far_peer, device_id_type=MESH,
        )

    def z_copy(direction, k):
        return pltpu.make_async_remote_copy(
            src_ref=zsend.at[direction, k], dst_ref=zgot.at[direction, k],
            send_sem=z_s.at[direction, k], recv_sem=z_r.at[direction, k],
            device_id=z_peers[direction], device_id_type=MESH,
        )

    weight_copy = pltpu.make_async_remote_copy(
        src_ref=sw.at[0], dst_ref=swfar, send_sem=w_sem.at[0], recv_sem=w_sem.at[1],
        device_id=far_peer, device_id_type=MESH,
    )
    for t in range(8):
        near_copy(lax.rem(t + 4 * odd, 8)).start()
        if t < 4:
            far_copy(t).start()

    def send_edges(t, carry):
        k = block_of(t)
        for c in range(3):
            for side in range(2):
                edge = jnp.dot(ends, planes[c, side, rows_of(k), :], preferred_element_type=F32).astype(BF)
                at = (2 * c + side) * 16
                zsend[0, k, at : at + 16, :] = edge[:16]
                zsend[1, k, at : at + 16, :] = edge[16:]
        z_copy(0, k).start()
        z_copy(1, k).start()
        return carry

    lax.fori_loop(0, 8, send_edges, 0)
    weight_copy.start()
    for k in range(8):
        for side in range(2):
            wide = weighted_columns(sw[side], k * 16, 16)
            for c in range(3):
                here = planes[c, side, PAD + k * CH : PAD + (k + 1) * CH, :].astype(F32)
                at = c * PT + side * CH
                turned[k, :, at : at + CH] = (here * wide).astype(BF).T

    def dot(step, buffer, tested):
        cols = pl.ds(pl.multiple_of(step * 256, 256), 256)
        total[:, cols] += lax.dot_general(
            tested, spread[buffer][...], (((1,), (1,)), ((), ())), preferred_element_type=F32
        )

    def run(first, tested, terms):
        first()
        terms(0, spread[0])

        def body(m, carry):
            dot(2 * m, 0, tested())
            terms(2 * m + 1, spread[1])
            dot(2 * m + 1, 1, tested())
            terms(2 * m + 2, spread[0])
            return carry

        lax.fori_loop(0, 3, body, 0)
        dot(6, 0, tested())
        terms(7, spread[1])

    def prepare(t, b, with_far):
        k = block_of(t)
        g = grads[b]
        flipped = [[], []]
        for side in range(2):
            lanes = slice(side * CH, (side + 1) * CH)
            for c in range(3):
                at = (2 * c + side) * 16
                stacked = jnp.concatenate(
                    [
                        planes[c, side, rows_of(k), :],
                        planes[c, side, pl.ds(pl.multiple_of(k * CH, 16), 16), :],
                        planes[c, side, pl.ds(pl.multiple_of(PAD + (k + 1) * CH, 16), 16), :],
                        zgot[1, k, at : at + 16, :],
                        zgot[0, k, at : at + 16, :],
                        jnp.zeros((64, M), BF),
                    ],
                    axis=0,
                ).T
                both = jnp.dot(stacked, stencil[...], preferred_element_type=F32)
                g[3 + c, :, lanes] = both[:, :CH]
                g[6 + c, :, lanes] = both[:, CH:]
                flipped[side].append(stacked[:, :CH])
            pk = jnp.dot(sel[...], jnp.concatenate(flipped[side], axis=0), preferred_element_type=F32)
            for r in range(3 * JW):
                picks[b][r, :, lanes] = jnp.broadcast_to(pk[r : r + 1], (8, CH))
        for c in range(3):
            inner = flipped[1][c].astype(F32)
            if with_far:
                inner = inner - far[t - 4, c].T.astype(F32)
            g[c, :, :CH] = inner
            g[c, :, CH:] = near[k, c].T.astype(F32) - flipped[0][c].astype(F32)

    def terms(b, step, target):
        g, pk = grads[b], picks[b]
        scale = []
        for h in range(2):
            p = [pk[d * JW + 2 * step + h] for d in range(3)]
            scale.append([jnp.concatenate([v, v], axis=0) for v in p])
        for c in range(3):
            for u in range(8):
                tile = slice(u * 16, u * 16 + 16)
                gx_, gy_, gz_ = g[c, tile, :], g[3 + c, tile, :], g[6 + c, tile, :]
                for h in range(2):
                    px, py, pz = scale[h]
                    value = px * gx_ + py * gy_ + pz * gz_
                    target[h * M + u * 16 : h * M + u * 16 + 16, c * PT : (c + 1) * PT] = value.astype(BF)

    def pair(u, carry, with_far):
        for t in (2 * u, 2 * u + 1):
            near_copy(block_of(t)).wait_recv()
            z_copy(0, block_of(t)).wait_recv()
            z_copy(1, block_of(t)).wait_recv()
            if with_far:
                far_copy(t - 4).wait_recv()
        for b in range(2):
            t = 2 * u + b
            before = block_of(lax.rem(t + 7, 8))

            def first(t=t, b=b, before=before):
                prepare(t, b, with_far)
                dot(7, 1, turned[before])

            run(first, lambda t=t: turned[block_of(t)], functools.partial(terms, b))
        return carry

    lax.fori_loop(0, 2, functools.partial(pair, with_far=False), 0)
    lax.fori_loop(2, 4, functools.partial(pair, with_far=True), 0)

    weight_copy.wait_recv()
    foreign = swfar[...]
    foreign = jnp.where(odd == 1, pltpu.roll(foreign, LV // 2, 1), foreign)

    def prepare_cross(v):
        wide = [weighted_columns(foreign, v * 32 + 16 * h, 16) for h in range(2)]
        pk = []
        for h in range(2):
            mine = 2 * v + h + 4 * odd
            for c in range(3):
                here = far[2 * v + h, c]
                if c == 0:
                    pk.append(jnp.dot(self_[...], here.T, preferred_element_type=F32).astype(BF))
                at = c * PT + h * CH
                cross_tested[v, :, at : at + CH] = (here.astype(F32) * wide[h]).astype(BF).T
                grads[v][c, :, h * CH : (h + 1) * CH] = planes[c, 0, rows_of(mine), :].T.astype(F32)
            for j in range(JW):
                picks[v][j, :, h * CH : (h + 1) * CH] = jnp.broadcast_to(
                    pk[h][j : j + 1].astype(F32), (8, CH)
                )

    def cross_terms(v, step, target):
        scale = []
        for h in range(2):
            p = picks[v][2 * step + h].astype(BF)
            scale.append(jnp.concatenate([p, p], axis=0))
        for c in range(3):
            for u in range(8):
                tile = grads[v][c, u * 16 : u * 16 + 16, :].astype(BF)
                for h in range(2):
                    target[h * M + u * 16 : h * M + u * 16 + 16, c * PT : (c + 1) * PT] = scale[h] * tile

    for v in range(2):

        def first(v=v):
            prepare_cross(v)
            dot(7, 1, turned[block_of(7)] if v == 0 else cross_tested[0])

        run(first, lambda v=v: cross_tested[v], functools.partial(cross_terms, v))
    dot(7, 1, cross_tested[1])

    for q in range(16):
        for low in range(2):
            owner = (q // 4) * 8 + low * 4 + q % 4
            out[q, low * 4 : low * 4 + 4, :] = total[owner * 4 : owner * 4 + 4, :]
    for k in range(8):
        near_copy(k).wait_send()
        z_copy(0, k).wait_send()
        z_copy(1, k).wait_send()
        if k < 4:
            far_copy(k).wait_send()
    weight_copy.wait_send()


def reduce_kernel(part, out, pair, send, got, column, stack, whole, asend, arecv, bsend, brecv, csend, crecv, dsem):
    gx, gz = lax.axis_index("gx"), lax.axis_index("gz")
    core, zh = lax.rem(gx, 2), gx // 2
    x, low, y = gz // 8, lax.rem(gz // 4, 2), lax.rem(gz, 4)
    q, z = x * 4 + y, zh * 2 + low
    partner = (gx + 1 - 2 * core, gz)

    def plane_peer(p):
        return (gx, (p // 4) * 8 + low * 4 + lax.rem(p, 4))

    def column_peer(p):
        return ((p // 2) * 2 + core, x * 8 + lax.rem(p, 2) * 4 + y)

    barrier = pltpu.get_barrier_semaphore()
    peers = [partner]
    peers += [plane_peer(lax.rem(q + d, 16)) for d in range(1, 16)]
    peers += [column_peer(lax.rem(z + d, 8)) for d in range(1, 8)]
    for peer in peers:
        pl.semaphore_signal(barrier, inc=1, device_id=peer, device_id_type=MESH)
    pl.semaphore_wait(barrier, len(peers))

    width = 8 * M
    own = pl.ds(pl.multiple_of(core * width, width), width)
    theirs = pl.ds(pl.multiple_of((1 - core) * width, width), width)

    def pair_copy(g):
        quarter = pl.ds(g * 4, 4)
        return pltpu.make_async_remote_copy(
            src_ref=part.at[quarter, :, theirs],
            dst_ref=pair.at[quarter],
            send_sem=asend.at[g],
            recv_sem=arecv.at[g],
            device_id=partner,
            device_id_type=MESH,
        )

    def plane_copy(dest, slot):
        return pltpu.make_async_remote_copy(
            src_ref=send.at[dest],
            dst_ref=got.at[slot],
            send_sem=bsend.at[dest],
            recv_sem=brecv.at[slot],
            device_id=plane_peer(dest),
            device_id_type=MESH,
        )

    def column_copy(dest, slot):
        return pltpu.make_async_remote_copy(
            src_ref=column.at[lax.rem(dest, 2)],
            dst_ref=stack.at[slot],
            send_sem=csend.at[dest],
            recv_sem=crecv.at[slot],
            device_id=column_peer(dest),
            device_id_type=MESH,
        )

    for g in range(4):
        pair_copy(g).start()
    for g in range(4):
        pair_copy(g).wait_recv()
        for b in range(g * 4, g * 4 + 4):
            send[b] = (part[b, :, own] + pair[b]).astype(BF)

            @pl.when(b != q)
            def _(b=b):
                plane_copy(b, q).start()

    total = send[q].astype(F32)
    for d in range(1, 16):
        p = lax.rem(q + d, 16)
        plane_copy(p, p).wait_recv()
        total = total + got[p].astype(F32)
    column[0] = total[:4]
    column[1] = total[4:]
    for d in (4, 3, 5, 2, 6, 1, 7):
        column_copy(lax.rem(z + d, 8), z).start()
    stack[z] = column[low]
    for d in range(1, 8):
        p = lax.rem(z + d, 8)
        column_copy(p, p).wait_recv()
    mine = stack[0]
    for p in range(1, 8):
        mine = mine + stack[p]
    for j in range(8):
        whole[core * 8 + j] = mine[:, j * M : (j + 1) * M]
    block = whole.at[pl.ds(core * 8, 8)]
    last = pltpu.make_async_remote_copy(
        src_ref=block, dst_ref=block, send_sem=dsem.at[0], recv_sem=dsem.at[1],
        device_id=partner, device_id_type=MESH,
    )
    last.start()
    for g in range(4):
        pair_copy(g).wait_send()
    for d in range(1, 16):
        plane_copy(lax.rem(q + d, 16), q).wait_send()
    for d in range(1, 8):
        column_copy(lax.rem(z + d, 8), z).wait_send()
    last.wait()
    out[...] = whole[...]


VM = pl.BlockSpec(memory_space=pltpu.VMEM)
SM = pl.BlockSpec(memory_space=pltpu.SMEM)
HB = pl.BlockSpec(memory_space=pl.ANY)


def local(modes, weights, counts, mode_index):
    part = pl.pallas_call(
        local_kernel,
        out_shape=jax.ShapeDtypeStruct((16, 8, JW * M), F32),
        in_specs=[HB, VM, SM, SM],
        out_specs=VM,
        scratch_shapes=[
            pltpu.VMEM((M, JW * M), F32),
            pltpu.VMEM((3, 2, ROWS + 2 * PAD, M), BF),
            pltpu.VMEM((8, 3, CH, M), BF),
            pltpu.VMEM((4, 3, CH, M), BF),
            pltpu.VMEM((2, 8, 96, M), BF),
            pltpu.VMEM((2, 8, 96, M), BF),
            pltpu.VMEM((2, CZ, LV), F32),
            pltpu.VMEM((CZ, LV), F32),
            pltpu.VMEM((8, M, 3 * PT), BF),
            pltpu.VMEM((2, M, 3 * PT), BF),
            [pltpu.VMEM((9, M, PT), F32)] * 2,
            [pltpu.VMEM((3 * JW, 8, PT), F32)] * 2,
            [pltpu.VMEM((2 * M, 3 * PT), BF)] * 2,
            pltpu.VMEM((PT, PT), BF),
            pltpu.VMEM((3 * JW, 3 * M), BF),
            pltpu.VMEM((JW, M), BF),
            pltpu.SemaphoreType.DMA((6,)),
            pltpu.SemaphoreType.DMA((8,)),
            pltpu.SemaphoreType.DMA((8,)),
            pltpu.SemaphoreType.DMA((4,)),
            pltpu.SemaphoreType.DMA((4,)),
            pltpu.SemaphoreType.DMA((2, 8)),
            pltpu.SemaphoreType.DMA((2, 8)),
            pltpu.SemaphoreType.DMA((2,)),
        ],
        compiler_params=pltpu.CompilerParams(
            vmem_limit_bytes=40 << 20, collective_id=1, has_side_effects=True
        ),
    )(modes.reshape(3, 2, ROWS, M), jnp.swapaxes(weights, 1, 2), counts, mode_index)

    return pl.pallas_call(
        reduce_kernel,
        out_shape=jax.ShapeDtypeStruct((JW, 4, M), F32),
        in_specs=[VM],
        out_specs=VM,
        scratch_shapes=[
            pltpu.VMEM((16, 8, 8 * M), F32),
            pltpu.VMEM((16, 8, 8 * M), BF),
            pltpu.VMEM((16, 8, 8 * M), BF),
            pltpu.VMEM((2, 4, 8 * M), F32),
            pltpu.VMEM((8, 4, 8 * M), F32),
            pltpu.VMEM((JW, 4, M), F32),
            pltpu.SemaphoreType.DMA((4,)),
            pltpu.SemaphoreType.DMA((4,)),
            pltpu.SemaphoreType.DMA((16,)),
            pltpu.SemaphoreType.DMA((16,)),
            pltpu.SemaphoreType.DMA((8,)),
            pltpu.SemaphoreType.DMA((8,)),
            pltpu.SemaphoreType.DMA((2,)),
        ],
        compiler_params=pltpu.CompilerParams(collective_id=0, has_side_effects=True),
    )(part)


def solution(mesh):
    placed = (P(None, "gx", None, "gz", None), P("gx", None, "gz"), P(("gx", "gz")), P())
    return jax.shard_map(
        local, mesh=mesh, in_specs=placed, out_specs=P(None, "gz", None), check_vma=False
    )
```

time: 74.1 us -> 70.4 us (0.950)
  Pallas kernels: 50 us -> 64.3 us
  starting transfers between devices: 11.7 us -> 0 us
  waiting for transfers between devices: 3.98 us -> 0 us
  local copies, waits for them, and re-layouts: 7.44 us -> 5.09 us
    ppermute x5 -> x0, starting transfers between devices: 11.7 us -> none  [the longest x1 5.68 us: local(): zhi = lax.ppermute(modes[:, :, :, 0, :], 'gz', down)]
    pallas_call x2 -> x1, Pallas kernels: 25.5 us -> 36.8 us  [local(): pl.pallas_call(local_kernel, out_shape=jax.ShapeDtypeStruct((16, 8, JW *...]
    ppermute x5 -> x0, waiting for transfers between devices: 3.98 us -> none  [the longest x1 3.9 us: local(): zhi = lax.ppermute(modes[:, :, :, 0, :], 'gz', down)]
    pallas_call x1, Pallas kernels: 24.4 us -> 27.5 us  [local(): pl.pallas_call(reduce_kernel, out_shape=jax.ShapeDtypeStruct((JW, 4, M),...]
    squeeze x2 -> x0, local copies, waits for them, and re-layouts: 2.27 us -> none  [the longest x1 2.19 us: local(): lax.dynamic_index_in_dim(flat, 1 - odd, 1, keepdims=False)]
    unnamed x11 -> x9, local copies, waits for them, and re-layouts: 3.77 us -> 5.09 us
    reshape x1 -> x0, local copies, waits for them, and re-layouts: 0.81 us -> none  [local(): far = lax.ppermute(sent.reshape(3, HALF, M), 'gx', across)]
  transfers between devices with their start and end apart: 5 -> 0, of which waited for: 2 -> 0; matrix products, arithmetic and copies ran while one was open for 4% -> 0% of each run, Pallas kernels for 25% -> 0%
where the time goes in v3:
time: 70.4 us; the launch traced here: 70.1 us
  Pallas kernels  64.3 us (91%)
  local copies, waits for them, and re-layouts  5.09 us (7%)
    pallas_call x1, Pallas kernels, local(): pl.pallas_call(local_kernel, out_shape=jax.ShapeDtypeStruct((16, 8, JW *...  36.8 us
    pallas_call x1, Pallas kernels, local(): pl.pallas_call(reduce_kernel, out_shape=jax.ShapeDtypeStruct((JW, 4, M),...  27.5 us
    unnamed x9, local copies, waits for them, and re-layouts  5.09 us

profile of v3, /device:TPU:1, one launch (start us, length us, event | category | flops | bytes accessed | tf_op | source)
XLA Modules:
  0.0 70.1 jit_solution(6976690202386051574)
XLA Ops:
  0.7 0.0 copy-start.1
  0.7 1.4 %copy-done.1 = bf16[3,2,128,8,128]{4,3,2,1,0:T(8,128)(2,1)S(1)} copy-done((bf16[3,2,128,8,128]{4,3,2,1,0:T(8,128)(2,1)S(1)}, bf16[3,2,128,8,128]{4,3,2,1,0:T(8,128)(2,1)}, u32[]{:S(2)}) %copy-start.1) | copy-done | bytes 1572888
  2.1 0.0 copy-start.2
  2.1 0.7 copy-done.2
  2.8 0.0 copy-start.3
  2.8 0.7 copy-done.3
  3.4 36.8 %shard_map.46.part = f32[16,8,2048]{2,1,0:T(8,128)S(1)} custom-call(bf16[3,2,1024,128]{3,2,1,0:T(8,128)(2,1)S(1)} %bitcast.2, f32[2,8,128]{2,1,0:T(8,128)S(1)} %bitcast.3, s32[1]{0:T(128)S(6)} %copy.6.counts, s32[16]{0:T(128)S(1)} %copy-done.3), custom_call_target="tpu_custom_call" | custom-call | tf_op jit(solution)/shard_map/pallas_call | solution.py:415
  40.3 0.0 copy-start
  40.3 1.0 %copy-done = f32[16,8,2048]{2,1,0:T(8,128)} copy-done((f32[16,8,2048]{2,1,0:T(8,128)}, f32[16,8,2048]{2,1,0:T(8,128)S(1)}, u32[]{:S(2)}) %copy-start) | copy-done | bytes 1048600
  41.2 27.5 %shard_map.47 = f32[16,4,128]{2,1,0:T(4,128)} custom-call(f32[16,8,2048]{2,1,0:T(8,128)} %copy-done), custom_call_target="tpu_custom_call" | custom-call | tf_op jit(solution)/shard_map/pallas_call | solution.py:451
  68.7 1.4 %copy.7 = f32[16,4,128]{2,1,0:T(4,128)} copy(f32[16,4,128]{2,1,0:T(4,128)} %shard_map.47) | data formatting | bytes 65536
Async XLA Ops:
  0.7 1.4 %copy-start.1 = (bf16[3,2,128,8,128]{4,3,2,1,0:T(8,128)(2,1)S(1)}, bf16[3,2,128,8,128]{4,3,2,1,0:T(8,128)(2,1)}, u32[]{:S(2)}) copy-start(bf16[3,2,128,8,128]{4,3,2,1,0:T(8,128)(2,1)} %param.4) | copy-start | bytes 4718596
  2.1 0.7 copy-start.2
  2.8 0.7 copy-start.3
  40.3 1.0 %copy-start = (f32[16,8,2048]{2,1,0:T(8,128)}, f32[16,8,2048]{2,1,0:T(8,128)S(1)}, u32[]{:S(2)}) copy-start(f32[16,8,2048]{2,1,0:T(8,128)S(1)} %shard_map.46.part) | copy-start | bytes 3145732

commit v4 on v3

--- a/solution.py
+++ b/solution.py
@@ -62,10 +62,129 @@
     return jnp.where(col == lax.rem(row, 16) * CZ + (row // 16) * (CZ - 1), 1.0, 0.0).astype(BF)
 
 
+def place():
+    gx, gz = lax.axis_index("gx"), lax.axis_index("gz")
+    core, zh = lax.rem(gx, 2), gx // 2
+    x, low, y = gz // 8, lax.rem(gz // 4, 2), lax.rem(gz, 4)
+    return gx, gz, core, x, low, y, x * 4 + y, zh * 2 + low
+
+
+def plane_peer(p):
+    gx, _, _, _, low, _, _, _ = place()
+    return (gx, (p // 4) * 8 + low * 4 + lax.rem(p, 4))
+
+
+def column_peer(p):
+    _, _, core, x, _, y, _, _ = place()
+    return ((p // 2) * 2 + core, x * 8 + lax.rem(p, 2) * 4 + y)
+
+
+def reduction_peers():
+    _, _, _, _, _, _, q, z = place()
+    return [plane_peer(lax.rem(q + d, 16)) for d in range(1, 16)] + [
+        column_peer(lax.rem(z + d, 8)) for d in range(1, 8)
+    ]
+
+
+def reduce_parts(
+    total, out, part, pair, send, got, column, stack, whole, asend, arecv, bsend, brecv, csend, crecv, dsem
+):
+    gx, gz, core, x, low, y, q, z = place()
+    partner = (gx + 1 - 2 * core, gz)
+
+    width = 8 * M
+    own = pl.ds(pl.multiple_of(core * width, width), width)
+    theirs = pl.ds(pl.multiple_of((1 - core) * width, width), width)
+
+    def pair_copy(g):
+        quarter = pl.ds(g * 4, 4)
+        return pltpu.make_async_remote_copy(
+            src_ref=part.at[quarter, :, theirs],
+            dst_ref=pair.at[quarter],
+            send_sem=asend.at[g],
+            recv_sem=arecv.at[g],
+            device_id=partner,
+            device_id_type=MESH,
+        )
+
+    def plane_copy(dest, slot):
+        return pltpu.make_async_remote_copy(
+            src_ref=send.at[dest],
+            dst_ref=got.at[slot],
+            send_sem=bsend.at[dest],
+            recv_sem=brecv.at[slot],
+            device_id=plane_peer(dest),
+            device_id_type=MESH,
+        )
+
+    def column_copy(dest, slot):
+        return pltpu.make_async_remote_copy(
+            src_ref=column.at[lax.rem(dest, 2)],
+            dst_ref=stack.at[slot],
+            send_sem=csend.at[dest],
+            recv_sem=crecv.at[slot],
+            device_id=column_peer(dest),
+            device_id_type=MESH,
+        )
+
+    for g in range(4):
+        for b in range(g * 4, g * 4 + 4):
+            for half in range(2):
+                owner = (b // 4) * 8 + half * 4 + b % 4
+                part[b, half * 4 : half * 4 + 4, :] = total[owner * 4 : owner * 4 + 4, :]
+        pair_copy(g).start()
+    for g in range(4):
+        pair_copy(g).wait_recv()
+        for b in range(g * 4, g * 4 + 4):
+            send[b] = (part[b, :, own] + pair[b]).astype(BF)
+
+            @pl.when(b != q)
+            def _(b=b):
+                plane_copy(b, q).start()
+
+    mine = send[q].astype(F32)
+    for d in range(1, 16):
+        p = lax.rem(q + d, 16)
+        plane_copy(p, p).wait_recv()
+        mine = mine + got[p].astype(F32)
+    column[0] = mine[:4]
+    column[1] = mine[4:]
+    for d in (4, 3, 5, 2, 6, 1, 7):
+        column_copy(lax.rem(z + d, 8), z).start()
+    stack[z] = column[low]
+    for d in range(1, 8):
+        p = lax.rem(z + d, 8)
+        column_copy(p, p).wait_recv()
+    mine = stack[0]
+    for p in range(1, 8):
+        mine = mine + stack[p]
+    for j in range(8):
+        whole[core * 8 + j] = mine[:, j * M : (j + 1) * M]
+    block = whole.at[pl.ds(core * 8, 8)]
+    last = pltpu.make_async_remote_copy(
+        src_ref=block, dst_ref=block, send_sem=dsem.at[0], recv_sem=dsem.at[1],
+        device_id=partner, device_id_type=MESH,
+    )
+    last.start()
+    last.wait_recv()
+    out[...] = whole[...]
+
+    def finish():
+        for g in range(4):
+            pair_copy(g).wait_send()
+        for d in range(1, 16):
+            plane_copy(lax.rem(q + d, 16), q).wait_send()
+        for d in range(1, 8):
+            column_copy(lax.rem(z + d, 8), z).wait_send()
+        last.wait_send()
+
+    return finish
+
+
 def local_kernel(
     modes, weights, counts, idx, out,
-    total, planes, near, far, zsend, zgot, sw, swfar, turned, cross_tested, grads, picks, spread, stencil, sel, self_,
-    local_sem, near_s, near_r, far_s, far_r, z_s, z_r, w_sem,
+    weights_in, total, planes, near, far, zsend, zgot, sw, swfar, turned, cross_tested, grads, picks, spread, stencil, sel, self_,
+    local_sem, near_s, near_r, far_s, far_r, z_s, z_r, w_sem, *reduction,
 ):
     gx, gz = lax.axis_index("gx"), lax.axis_index("gz")
     odd = lax.rem(gx, 2)
@@ -74,6 +193,11 @@
     far_peer = (lax.rem(gx + 7 + 2 * odd, 8), gz)
     z_peers = ((gx, lax.rem(gz + 31, 32)), (gx, lax.rem(gz + 1, 32)))
 
+    barrier = pltpu.get_barrier_semaphore()
+    peers = [near_peer, far_peer, *z_peers, *reduction_peers()]
+    for peer in peers:
+        pl.semaphore_signal(barrier, inc=1, device_id=peer, device_id_type=MESH)
+    small = [pltpu.make_async_copy(weights, weights_in, local_sem.at[6])]
     copies = []
     for c in range(3):
         for side in range(2):
@@ -83,17 +207,17 @@
                     modes.at[c, which], planes.at[c, side, pl.ds(PAD, ROWS)], local_sem.at[2 * c + side]
                 )
             )
-            copies[-1].start()
-    barrier = pltpu.get_barrier_semaphore()
-    for peer in (near_peer, far_peer, *z_peers):
-        pl.semaphore_signal(barrier, inc=1, device_id=peer, device_id_type=MESH)
+    for copy in (*small, *copies):
+        copy.start()
     for c in range(3):
         for side in range(2):
             planes[c, side, pl.ds(0, PAD), :] = jnp.zeros((PAD, M), BF)
             planes[c, side, pl.ds(PAD + ROWS, PAD), :] = jnp.zeros((PAD, M), BF)
+    for copy in small:
+        copy.wait()
     for side in range(2):
         which = odd if side == 0 else 1 - odd
-        w = weights[which]
+        w = weights_in[which]
         sw[side] = jnp.where(iota((CZ, LV), 1) < counts[0], w, jnp.zeros_like(w))
     stencil[...] = stencil_matrix()
     sel[...] = pick_rows(idx, (sign, 0.5, 0.5))
@@ -103,7 +227,6 @@
     ends = select_rows()
     for copy in copies:
         copy.wait()
-    pl.semaphore_wait(barrier, 4)
 
     def block_of(t):
         return lax.rem(t + 4 * (1 - odd), 8)
@@ -134,10 +257,6 @@
         src_ref=sw.at[0], dst_ref=swfar, send_sem=w_sem.at[0], recv_sem=w_sem.at[1],
         device_id=far_peer, device_id_type=MESH,
     )
-    for t in range(8):
-        near_copy(lax.rem(t + 4 * odd, 8)).start()
-        if t < 4:
-            far_copy(t).start()
 
     def send_edges(t, carry):
         k = block_of(t)
@@ -147,11 +266,14 @@
                 at = (2 * c + side) * 16
                 zsend[0, k, at : at + 16, :] = edge[:16]
                 zsend[1, k, at : at + 16, :] = edge[16:]
-        z_copy(0, k).start()
-        z_copy(1, k).start()
         return carry
 
     lax.fori_loop(0, 8, send_edges, 0)
+    pl.semaphore_wait(barrier, len(peers))
+    for t in range(8):
+        near_copy(lax.rem(t + 4 * odd, 8)).start()
+        z_copy(0, block_of(t)).start()
+        z_copy(1, block_of(t)).start()
     weight_copy.start()
     for k in range(8):
         for side in range(2):
@@ -160,6 +282,9 @@
                 here = planes[c, side, PAD + k * CH : PAD + (k + 1) * CH, :].astype(F32)
                 at = c * PT + side * CH
                 turned[k, :, at : at + CH] = (here * wide).astype(BF).T
+
+    far_copy(0).start()
+    far_copy(1).start()
 
     def dot(step, buffer, tested):
         cols = pl.ds(pl.multiple_of(step * 256, 256), 256)
@@ -237,6 +362,13 @@
             z_copy(1, block_of(t)).wait_recv()
             if with_far:
                 far_copy(t - 4).wait_recv()
+        if not with_far:
+
+            @pl.when(u == 0)
+            def _():
+                far_copy(2).start()
+                far_copy(3).start()
+
         for b in range(2):
             t = 2 * u + b
             before = block_of(lax.rem(t + 7, 8))
@@ -292,10 +424,7 @@
         run(first, lambda v=v: cross_tested[v], functools.partial(cross_terms, v))
     dot(7, 1, cross_tested[1])
 
-    for q in range(16):
-        for low in range(2):
-            owner = (q // 4) * 8 + low * 4 + q % 4
-            out[q, low * 4 : low * 4 + 4, :] = total[owner * 4 : owner * 4 + 4, :]
+    finish = reduce_parts(total, out, *reduction)
     for k in range(8):
         near_copy(k).wait_send()
         z_copy(0, k).wait_send()
@@ -303,107 +432,7 @@
         if k < 4:
             far_copy(k).wait_send()
     weight_copy.wait_send()
-
-
-def reduce_kernel(part, out, pair, send, got, column, stack, whole, asend, arecv, bsend, brecv, csend, crecv, dsem):
-    gx, gz = lax.axis_index("gx"), lax.axis_index("gz")
-    core, zh = lax.rem(gx, 2), gx // 2
-    x, low, y = gz // 8, lax.rem(gz // 4, 2), lax.rem(gz, 4)
-    q, z = x * 4 + y, zh * 2 + low
-    partner = (gx + 1 - 2 * core, gz)
-
-    def plane_peer(p):
-        return (gx, (p // 4) * 8 + low * 4 + lax.rem(p, 4))
-
-    def column_peer(p):
-        return ((p // 2) * 2 + core, x * 8 + lax.rem(p, 2) * 4 + y)
-
-    barrier = pltpu.get_barrier_semaphore()
-    peers = [partner]
-    peers += [plane_peer(lax.rem(q + d, 16)) for d in range(1, 16)]
-    peers += [column_peer(lax.rem(z + d, 8)) for d in range(1, 8)]
-    for peer in peers:
-        pl.semaphore_signal(barrier, inc=1, device_id=peer, device_id_type=MESH)
-    pl.semaphore_wait(barrier, len(peers))
-
-    width = 8 * M
-    own = pl.ds(pl.multiple_of(core * width, width), width)
-    theirs = pl.ds(pl.multiple_of((1 - core) * width, width), width)
-
-    def pair_copy(g):
-        quarter = pl.ds(g * 4, 4)
-        return pltpu.make_async_remote_copy(
-            src_ref=part.at[quarter, :, theirs],
-            dst_ref=pair.at[quarter],
-            send_sem=asend.at[g],
-            recv_sem=arecv.at[g],
-            device_id=partner,
-            device_id_type=MESH,
-        )
-
-    def plane_copy(dest, slot):
-        return pltpu.make_async_remote_copy(
-            src_ref=send.at[dest],
-            dst_ref=got.at[slot],
-            send_sem=bsend.at[dest],
-            recv_sem=brecv.at[slot],
-            device_id=plane_peer(dest),
-            device_id_type=MESH,
-        )
-
-    def column_copy(dest, slot):
-        return pltpu.make_async_remote_copy(
-            src_ref=column.at[lax.rem(dest, 2)],
-            dst_ref=stack.at[slot],
-            send_sem=csend.at[dest],
-            recv_sem=crecv.at[slot],
-            device_id=column_peer(dest),
-            device_id_type=MESH,
-        )
-
-    for g in range(4):
-        pair_copy(g).start()
-    for g in range(4):
-        pair_copy(g).wait_recv()
-        for b in range(g * 4, g * 4 + 4):
-            send[b] = (part[b, :, own] + pair[b]).astype(BF)
-
-            @pl.when(b != q)
-            def _(b=b):
-                plane_copy(b, q).start()
-
-    total = send[q].astype(F32)
-    for d in range(1, 16):
-        p = lax.rem(q + d, 16)
-        plane_copy(p, p).wait_recv()
-        total = total + got[p].astype(F32)
-    column[0] = total[:4]
-    column[1] = total[4:]
-    for d in (4, 3, 5, 2, 6, 1, 7):
-        column_copy(lax.rem(z + d, 8), z).start()
-    stack[z] = column[low]
-    for d in range(1, 8):
-        p = lax.rem(z + d, 8)
-        column_copy(p, p).wait_recv()
-    mine = stack[0]
-    for p in range(1, 8):
-        mine = mine + stack[p]
-    for j in range(8):
-        whole[core * 8 + j] = mine[:, j * M : (j + 1) * M]
-    block = whole.at[pl.ds(core * 8, 8)]
-    last = pltpu.make_async_remote_copy(
-        src_ref=block, dst_ref=block, send_sem=dsem.at[0], recv_sem=dsem.at[1],
-        device_id=partner, device_id_type=MESH,
-    )
-    last.start()
-    for g in range(4):
-        pair_copy(g).wait_send()
-    for d in range(1, 16):
-        plane_copy(lax.rem(q + d, 16), q).wait_send()
-    for d in range(1, 8):
-        column_copy(lax.rem(z + d, 8), z).wait_send()
-    last.wait()
-    out[...] = whole[...]
+    finish()
 
 
 VM = pl.BlockSpec(memory_space=pltpu.VMEM)
@@ -412,12 +441,13 @@
 
 
 def local(modes, weights, counts, mode_index):
-    part = pl.pallas_call(
+    return pl.pallas_call(
         local_kernel,
-        out_shape=jax.ShapeDtypeStruct((16, 8, JW * M), F32),
-        in_specs=[HB, VM, SM, SM],
+        out_shape=jax.ShapeDtypeStruct((JW, 4, M), F32),
+        in_specs=[HB, HB, SM, SM],
         out_specs=VM,
         scratch_shapes=[
+            pltpu.VMEM((2, CZ, LV), F32),
             pltpu.VMEM((M, JW * M), F32),
             pltpu.VMEM((3, 2, ROWS + 2 * PAD, M), BF),
             pltpu.VMEM((8, 3, CH, M), BF),
@@ -434,7 +464,7 @@
             pltpu.VMEM((PT, PT), BF),
             pltpu.VMEM((3 * JW, 3 * M), BF),
             pltpu.VMEM((JW, M), BF),
-            pltpu.SemaphoreType.DMA((6,)),
+            pltpu.SemaphoreType.DMA((7,)),
             pltpu.SemaphoreType.DMA((8,)),
             pltpu.SemaphoreType.DMA((8,)),
             pltpu.SemaphoreType.DMA((4,)),
@@ -442,18 +472,7 @@
             pltpu.SemaphoreType.DMA((2, 8)),
             pltpu.SemaphoreType.DMA((2, 8)),
             pltpu.SemaphoreType.DMA((2,)),
-        ],
-        compiler_params=pltpu.CompilerParams(
-            vmem_limit_bytes=40 << 20, collective_id=1, has_side_effects=True
-        ),
-    )(modes.reshape(3, 2, ROWS, M), jnp.swapaxes(weights, 1, 2), counts, mode_index)
-
-    return pl.pallas_call(
-        reduce_kernel,
-        out_shape=jax.ShapeDtypeStruct((JW, 4, M), F32),
-        in_specs=[VM],
-        out_specs=VM,
-        scratch_shapes=[
+            pltpu.VMEM((16, 8, JW * M), F32),
             pltpu.VMEM((16, 8, 8 * M), F32),
             pltpu.VMEM((16, 8, 8 * M), BF),
             pltpu.VMEM((16, 8, 8 * M), BF),
@@ -468,8 +487,10 @@
             pltpu.SemaphoreType.DMA((8,)),
             pltpu.SemaphoreType.DMA((2,)),
         ],
-        compiler_params=pltpu.CompilerParams(collective_id=0, has_side_effects=True),
-    )(part)
+        compiler_params=pltpu.CompilerParams(
+            vmem_limit_bytes=67043328, collective_id=0, has_side_effects=True
+        ),
+    )(modes.reshape(3, 2, ROWS, M), jnp.swapaxes(weights, 1, 2), counts, mode_index)
 
 
 def solution(mesh):

time: 70.4 us -> 58.5 us (0.83)
  Pallas kernels: 64.3 us -> 56.3 us
  local copies, waits for them, and re-layouts: 5.09 us -> 1.38 us
    pallas_call x2 -> x1, Pallas kernels: 64.3 us -> 56.3 us  [local(): pl.pallas_call(local_kernel, out_shape=jax.ShapeDtypeStruct((JW, 4, M), F...]
    unnamed x9 -> x1, local copies, waits for them, and re-layouts: 5.09 us -> 1.38 us
where the time goes in v4:
time: 58.5 us; the launch traced here: 58.3 us
  Pallas kernels  56.3 us (96%)
  local copies, waits for them, and re-layouts  1.38 us (2%)
  between operations  0.66 us (1%)
    pallas_call x1, Pallas kernels, local(): pl.pallas_call(local_kernel, out_shape=jax.ShapeDtypeStruct((JW, 4, M), F...  56.3 us
    unnamed x1, local copies, waits for them, and re-layouts  1.38 us

profile of v4, /device:TPU:1, one launch (start us, length us, event | category | flops | bytes accessed | tf_op | source)
XLA Modules:
  0.0 58.3 jit_solution(711197318076803882)
XLA Ops:
  0.7 56.3 %shard_map.46 = f32[16,4,128]{2,1,0:T(4,128)} custom-call(bf16[3,2,1024,128]{3,2,1,0:T(8,128)(2,1)} %bitcast.2, f32[2,8,128]{2,1,0:T(8,128)} %bitcast.3, s32[1]{0:T(128)S(6)} %copy.6.counts, s32[16]{0:T(128)} %idx.1), custom_call_target="tpu_custom_call" | custom-call | tf_op jit(solution)/shard_map/pallas_call | solution.py:444
  56.9 1.4 %copy.7 = f32[16,4,128]{2,1,0:T(4,128)} copy(f32[16,4,128]{2,1,0:T(4,128)} %shard_map.46) | data formatting | bytes 65536

commit v5 on v4

--- a/solution.py
+++ b/solution.py
@@ -223,7 +223,7 @@
     sel[...] = pick_rows(idx, (sign, 0.5, 0.5))
     self_[...] = pick_rows(idx, (sign,))
     total[...] = jnp.zeros_like(total)
-    spread[1][...] = jnp.zeros_like(spread[1])
+    spread[3][...] = jnp.zeros_like(spread[3])
     ends = select_rows()
     for copy in copies:
         copy.wait()
@@ -287,7 +287,7 @@
     far_copy(1).start()
 
     def dot(step, buffer, tested):
-        cols = pl.ds(pl.multiple_of(step * 256, 256), 256)
+        cols = slice(step * 256, step * 256 + 256)
         total[:, cols] += lax.dot_general(
             tested, spread[buffer][...], (((1,), (1,)), ((), ())), preferred_element_type=F32
         )
@@ -295,17 +295,9 @@
     def run(first, tested, terms):
         first()
         terms(0, spread[0])
-
-        def body(m, carry):
-            dot(2 * m, 0, tested())
-            terms(2 * m + 1, spread[1])
-            dot(2 * m + 1, 1, tested())
-            terms(2 * m + 2, spread[0])
-            return carry
-
-        lax.fori_loop(0, 3, body, 0)
-        dot(6, 0, tested())
-        terms(7, spread[1])
+        for step in range(7):
+            dot(step, step % 4, tested())
+            terms(step + 1, spread[(step + 1) % 4])
 
     def prepare(t, b, with_far):
         k = block_of(t)
@@ -375,7 +367,7 @@
 
             def first(t=t, b=b, before=before):
                 prepare(t, b, with_far)
-                dot(7, 1, turned[before])
+                dot(7, 3, turned[before])
 
             run(first, lambda t=t: turned[block_of(t)], functools.partial(terms, b))
         return carry
@@ -419,10 +411,10 @@
 
         def first(v=v):
             prepare_cross(v)
-            dot(7, 1, turned[block_of(7)] if v == 0 else cross_tested[0])
+            dot(7, 3, turned[block_of(7)] if v == 0 else cross_tested[0])
 
         run(first, lambda v=v: cross_tested[v], functools.partial(cross_terms, v))
-    dot(7, 1, cross_tested[1])
+    dot(7, 3, cross_tested[1])
 
     finish = reduce_parts(total, out, *reduction)
     for k in range(8):
@@ -460,7 +452,7 @@
             pltpu.VMEM((2, M, 3 * PT), BF),
             [pltpu.VMEM((9, M, PT), F32)] * 2,
             [pltpu.VMEM((3 * JW, 8, PT), F32)] * 2,
-            [pltpu.VMEM((2 * M, 3 * PT), BF)] * 2,
+            [pltpu.VMEM((2 * M, 3 * PT), BF)] * 4,
             pltpu.VMEM((PT, PT), BF),
             pltpu.VMEM((3 * JW, 3 * M), BF),
             pltpu.VMEM((JW, M), BF),

time: 58.5 us -> 55.1 us (0.942)
  Pallas kernels: 56.3 us -> 52.9 us
    pallas_call x1, Pallas kernels: 56.3 us -> 52.9 us  [local(): pl.pallas_call(local_kernel, out_shape=jax.ShapeDtypeStruct((JW, 4, M), F...]
where the time goes in v5:
time: 55.1 us; the launch traced here: 54.9 us
  Pallas kernels  52.9 us (96%)
  local copies, waits for them, and re-layouts  1.38 us (3%)
  between operations  0.66 us (1%)
    pallas_call x1, Pallas kernels, local(): pl.pallas_call(local_kernel, out_shape=jax.ShapeDtypeStruct((JW, 4, M), F...  52.9 us
    unnamed x1, local copies, waits for them, and re-layouts  1.38 us

profile of v5, /device:TPU:1, one launch (start us, length us, event | category | flops | bytes accessed | tf_op | source)
XLA Modules:
  0.0 54.9 jit_solution(6816904847578986366)
XLA Ops:
  0.7 52.9 %shard_map.46 = f32[16,4,128]{2,1,0:T(4,128)} custom-call(bf16[3,2,1024,128]{3,2,1,0:T(8,128)(2,1)} %bitcast.2, f32[2,8,128]{2,1,0:T(8,128)} %bitcast.3, s32[1]{0:T(128)S(6)} %copy.6.counts, s32[16]{0:T(128)} %idx.1), custom_call_target="tpu_custom_call" | custom-call | tf_op jit(solution)/shard_map/pallas_call | solution.py:436
  53.6 1.4 %copy.7 = f32[16,4,128]{2,1,0:T(4,128)} copy(f32[16,4,128]{2,1,0:T(4,128)} %shard_map.46) | data formatting | bytes 65536

commit v6 on v5

--- a/solution.py
+++ b/solution.py
@@ -222,8 +222,6 @@
     stencil[...] = stencil_matrix()
     sel[...] = pick_rows(idx, (sign, 0.5, 0.5))
     self_[...] = pick_rows(idx, (sign,))
-    total[...] = jnp.zeros_like(total)
-    spread[3][...] = jnp.zeros_like(spread[3])
     ends = select_rows()
     for copy in copies:
         copy.wait()
@@ -274,6 +272,8 @@
         near_copy(lax.rem(t + 4 * odd, 8)).start()
         z_copy(0, block_of(t)).start()
         z_copy(1, block_of(t)).start()
+    for p in range(4):
+        far_copy(p).start()
     weight_copy.start()
     for k in range(8):
         for side in range(2):
@@ -283,24 +283,13 @@
                 at = c * PT + side * CH
                 turned[k, :, at : at + CH] = (here * wide).astype(BF).T
 
-    far_copy(0).start()
-    far_copy(1).start()
-
-    def dot(step, buffer, tested):
-        cols = slice(step * 256, step * 256 + 256)
-        total[:, cols] += lax.dot_general(
-            tested, spread[buffer][...], (((1,), (1,)), ((), ())), preferred_element_type=F32
-        )
-
-    def run(first, tested, terms):
-        first()
-        terms(0, spread[0])
-        for step in range(7):
-            dot(step, step % 4, tested())
-            terms(step + 1, spread[(step + 1) % 4])
-
-    def prepare(t, b, with_far):
-        k = block_of(t)
+    def prepare(t):
+        k, b, with_far = block_of(t), t % 2, t >= 4
+        near_copy(k).wait_recv()
+        z_copy(0, k).wait_recv()
+        z_copy(1, k).wait_recv()
+        if with_far:
+            far_copy(t - 4).wait_recv()
         g = grads[b]
         flipped = [[], []]
         for side in range(2):
@@ -347,39 +336,11 @@
                     value = px * gx_ + py * gy_ + pz * gz_
                     target[h * M + u * 16 : h * M + u * 16 + 16, c * PT : (c + 1) * PT] = value.astype(BF)
 
-    def pair(u, carry, with_far):
-        for t in (2 * u, 2 * u + 1):
-            near_copy(block_of(t)).wait_recv()
-            z_copy(0, block_of(t)).wait_recv()
-            z_copy(1, block_of(t)).wait_recv()
-            if with_far:
-                far_copy(t - 4).wait_recv()
-        if not with_far:
-
-            @pl.when(u == 0)
-            def _():
-                far_copy(2).start()
-                far_copy(3).start()
-
-        for b in range(2):
-            t = 2 * u + b
-            before = block_of(lax.rem(t + 7, 8))
-
-            def first(t=t, b=b, before=before):
-                prepare(t, b, with_far)
-                dot(7, 3, turned[before])
-
-            run(first, lambda t=t: turned[block_of(t)], functools.partial(terms, b))
-        return carry
-
-    lax.fori_loop(0, 2, functools.partial(pair, with_far=False), 0)
-    lax.fori_loop(2, 4, functools.partial(pair, with_far=True), 0)
-
-    weight_copy.wait_recv()
-    foreign = swfar[...]
-    foreign = jnp.where(odd == 1, pltpu.roll(foreign, LV // 2, 1), foreign)
-
     def prepare_cross(v):
+        if v == 0:
+            weight_copy.wait_recv()
+        foreign = swfar[...]
+        foreign = jnp.where(odd == 1, pltpu.roll(foreign, LV // 2, 1), foreign)
         wide = [weighted_columns(foreign, v * 32 + 16 * h, 16) for h in range(2)]
         pk = []
         for h in range(2):
@@ -407,14 +368,35 @@
                 for h in range(2):
                     target[h * M + u * 16 : h * M + u * 16 + 16, c * PT : (c + 1) * PT] = scale[h] * tile
 
-    for v in range(2):
-
-        def first(v=v):
-            prepare_cross(v)
-            dot(7, 3, turned[block_of(7)] if v == 0 else cross_tested[0])
-
-        run(first, lambda v=v: cross_tested[v], functools.partial(cross_terms, v))
-    dot(7, 3, cross_tested[1])
+    stages = [
+        (functools.partial(prepare, t), functools.partial(terms, t % 2), lambda t=t: turned[block_of(t)])
+        for t in range(8)
+    ]
+    stages += [
+        (functools.partial(prepare_cross, v), functools.partial(cross_terms, v), lambda v=v: cross_tested[v])
+        for v in range(2)
+    ]
+    waiting = None
+    stages[0][0]()
+    for i, (_, form, tested) in enumerate(stages):
+        for step in range(8):
+            if waiting is not None:
+                waiting()
+
+            def waiting(step=step, tested=tested, fresh=i == 0):
+                value = lax.dot_general(
+                    tested(),
+                    spread[step % 4][...],
+                    (((1,), (1,)), ((), ())),
+                    preferred_element_type=F32,
+                )
+                cols = slice(step * 256, step * 256 + 256)
+                total[:, cols] = value if fresh else total[:, cols] + value
+
+            form(step, spread[step % 4])
+            if step == 3 and i + 1 < len(stages):
+                stages[i + 1][0]()
+    waiting()
 
     finish = reduce_parts(total, out, *reduction)
     for k in range(8):

time: 55.1 us -> 52.7 us (0.956)
  Pallas kernels: 52.9 us -> 50.4 us
    pallas_call x1, Pallas kernels: 52.9 us -> 50.4 us  [local(): pl.pallas_call(local_kernel, out_shape=jax.ShapeDtypeStruct((JW, 4, M), F...]
where the time goes in v6:
time: 52.7 us; the launch traced here: 52.5 us
  Pallas kernels  50.4 us (96%)
  local copies, waits for them, and re-layouts  1.38 us (3%)
  between operations  0.66 us (1%)
    pallas_call x1, Pallas kernels, local(): pl.pallas_call(local_kernel, out_shape=jax.ShapeDtypeStruct((JW, 4, M), F...  50.4 us
    unnamed x1, local copies, waits for them, and re-layouts  1.38 us

profile of v6, /device:TPU:1, one launch (start us, length us, event | category | flops | bytes accessed | tf_op | source)
XLA Modules:
  0.0 52.5 jit_solution(10288411233611262104)
XLA Ops:
  0.7 50.4 %shard_map.46 = f32[16,4,128]{2,1,0:T(4,128)} custom-call(bf16[3,2,1024,128]{3,2,1,0:T(8,128)(2,1)} %bitcast.2, f32[2,8,128]{2,1,0:T(8,128)} %bitcast.3, s32[1]{0:T(128)S(6)} %copy.6.counts, s32[16]{0:T(128)} %idx.1), custom_call_target="tpu_custom_call" | custom-call | tf_op jit(solution)/shard_map/pallas_call | solution.py:418
  51.1 1.4 %copy.7 = f32[16,4,128]{2,1,0:T(4,128)} copy(f32[16,4,128]{2,1,0:T(4,128)} %shard_map.46) | data formatting | bytes 65536

commit v7 on v6

--- a/solution.py
+++ b/solution.py
@@ -147,17 +147,17 @@
         p = lax.rem(q + d, 16)
         plane_copy(p, p).wait_recv()
         mine = mine + got[p].astype(F32)
-    column[0] = mine[:4]
-    column[1] = mine[4:]
+    column[0] = mine[:4].astype(BF)
+    column[1] = mine[4:].astype(BF)
     for d in (4, 3, 5, 2, 6, 1, 7):
         column_copy(lax.rem(z + d, 8), z).start()
     stack[z] = column[low]
     for d in range(1, 8):
         p = lax.rem(z + d, 8)
         column_copy(p, p).wait_recv()
-    mine = stack[0]
+    mine = stack[0].astype(F32)
     for p in range(1, 8):
-        mine = mine + stack[p]
+        mine = mine + stack[p].astype(F32)
     for j in range(8):
         whole[core * 8 + j] = mine[:, j * M : (j + 1) * M]
     block = whole.at[pl.ds(core * 8, 8)]
@@ -283,8 +283,8 @@
                 at = c * PT + side * CH
                 turned[k, :, at : at + CH] = (here * wide).astype(BF).T
 
-    def prepare(t):
-        k, b, with_far = block_of(t), t % 2, t >= 4
+    def prepare(t, b):
+        k, with_far = block_of(t), t >= 4
         near_copy(k).wait_recv()
         z_copy(0, k).wait_recv()
         z_copy(1, k).wait_recv()
@@ -336,7 +336,7 @@
                     value = px * gx_ + py * gy_ + pz * gz_
                     target[h * M + u * 16 : h * M + u * 16 + 16, c * PT : (c + 1) * PT] = value.astype(BF)
 
-    def prepare_cross(v):
+    def prepare_cross(v, b):
         if v == 0:
             weight_copy.wait_recv()
         foreign = swfar[...]
@@ -351,31 +351,32 @@
                     pk.append(jnp.dot(self_[...], here.T, preferred_element_type=F32).astype(BF))
                 at = c * PT + h * CH
                 cross_tested[v, :, at : at + CH] = (here.astype(F32) * wide[h]).astype(BF).T
-                grads[v][c, :, h * CH : (h + 1) * CH] = planes[c, 0, rows_of(mine), :].T.astype(F32)
+                grads[b][c, :, h * CH : (h + 1) * CH] = planes[c, 0, rows_of(mine), :].T.astype(F32)
             for j in range(JW):
-                picks[v][j, :, h * CH : (h + 1) * CH] = jnp.broadcast_to(
+                picks[b][j, :, h * CH : (h + 1) * CH] = jnp.broadcast_to(
                     pk[h][j : j + 1].astype(F32), (8, CH)
                 )
 
-    def cross_terms(v, step, target):
+    def cross_terms(b, step, target):
         scale = []
         for h in range(2):
-            p = picks[v][2 * step + h].astype(BF)
+            p = picks[b][2 * step + h].astype(BF)
             scale.append(jnp.concatenate([p, p], axis=0))
         for c in range(3):
             for u in range(8):
-                tile = grads[v][c, u * 16 : u * 16 + 16, :].astype(BF)
+                tile = grads[b][c, u * 16 : u * 16 + 16, :].astype(BF)
                 for h in range(2):
                     target[h * M + u * 16 : h * M + u * 16 + 16, c * PT : (c + 1) * PT] = scale[h] * tile
 
-    stages = [
-        (functools.partial(prepare, t), functools.partial(terms, t % 2), lambda t=t: turned[block_of(t)])
-        for t in range(8)
-    ]
-    stages += [
-        (functools.partial(prepare_cross, v), functools.partial(cross_terms, v), lambda v=v: cross_tested[v])
-        for v in range(2)
-    ]
+    stages = []
+    for kind, n in [(0, t) for t in range(6)] + [(1, 0), (0, 6), (0, 7), (1, 1)]:
+        b = len(stages) % 2
+        if kind == 0:
+            made, form = functools.partial(prepare, n, b), functools.partial(terms, b)
+            stages.append((made, form, lambda n=n: turned[block_of(n)]))
+        else:
+            made, form = functools.partial(prepare_cross, n, b), functools.partial(cross_terms, b)
+            stages.append((made, form, lambda n=n: cross_tested[n]))
     waiting = None
     stages[0][0]()
     for i, (_, form, tested) in enumerate(stages):
@@ -450,8 +451,8 @@
             pltpu.VMEM((16, 8, 8 * M), F32),
             pltpu.VMEM((16, 8, 8 * M), BF),
             pltpu.VMEM((16, 8, 8 * M), BF),
-            pltpu.VMEM((2, 4, 8 * M), F32),
-            pltpu.VMEM((8, 4, 8 * M), F32),
+            pltpu.VMEM((2, 4, 8 * M), BF),
+            pltpu.VMEM((8, 4, 8 * M), BF),
             pltpu.VMEM((JW, 4, M), F32),
             pltpu.SemaphoreType.DMA((4,)),
             pltpu.SemaphoreType.DMA((4,)),

time: 52.7 us -> 51.6 us (0.979)
  Pallas kernels: 50.4 us -> 49.4 us
    pallas_call x1, Pallas kernels: 50.4 us -> 49.4 us  [local(): pl.pallas_call(local_kernel, out_shape=jax.ShapeDtypeStruct((JW, 4, M), F...]
where the time goes in v7:
time: 51.6 us; the launch traced here: 51.4 us
  Pallas kernels  49.4 us (96%)
  local copies, waits for them, and re-layouts  1.38 us (3%)
  between operations  0.66 us (1%)
    pallas_call x1, Pallas kernels, local(): pl.pallas_call(local_kernel, out_shape=jax.ShapeDtypeStruct((JW, 4, M), F...  49.4 us
    unnamed x1, local copies, waits for them, and re-layouts  1.38 us

profile of v7, /device:TPU:1, one launch (start us, length us, event | category | flops | bytes accessed | tf_op | source)
XLA Modules:
  0.0 51.4 jit_solution(17370945617660574718)
XLA Ops:
  0.7 49.4 %shard_map.46 = f32[16,4,128]{2,1,0:T(4,128)} custom-call(bf16[3,2,1024,128]{3,2,1,0:T(8,128)(2,1)} %bitcast.2, f32[2,8,128]{2,1,0:T(8,128)} %bitcast.3, s32[1]{0:T(128)S(6)} %copy.6.counts, s32[16]{0:T(128)} %idx.1), custom_call_target="tpu_custom_call" | custom-call | tf_op jit(solution)/shard_map/pallas_call | solution.py:419
  50.0 1.4 %copy.7 = f32[16,4,128]{2,1,0:T(4,128)} copy(f32[16,4,128]{2,1,0:T(4,128)} %shard_map.46) | data formatting | bytes 65536

commit v8 on v7

--- a/solution.py
+++ b/solution.py
@@ -395,7 +395,7 @@
                 total[:, cols] = value if fresh else total[:, cols] + value
 
             form(step, spread[step % 4])
-            if step == 3 and i + 1 < len(stages):
+            if step == 5 and i + 1 < len(stages):
                 stages[i + 1][0]()
     waiting()
 

time: 51.6 us -> 51.5 us (level)
  no operation moved by 1% of the time
where the time goes in v8:
time: 51.5 us; the launch traced here: 51.3 us
  Pallas kernels  49.3 us (96%)
  local copies, waits for them, and re-layouts  1.38 us (3%)
  between operations  0.66 us (1%)
    pallas_call x1, Pallas kernels, local(): pl.pallas_call(local_kernel, out_shape=jax.ShapeDtypeStruct((JW, 4, M), F...  49.3 us
    unnamed x1, local copies, waits for them, and re-layouts  1.38 us

profile of v8, /device:TPU:1, one launch (start us, length us, event | category | flops | bytes accessed | tf_op | source)
XLA Modules:
  0.0 51.3 jit_solution(5123938656291702793)
XLA Ops:
  0.7 49.3 %shard_map.46 = f32[16,4,128]{2,1,0:T(4,128)} custom-call(bf16[3,2,1024,128]{3,2,1,0:T(8,128)(2,1)} %bitcast.2, f32[2,8,128]{2,1,0:T(8,128)} %bitcast.3, s32[1]{0:T(128)S(6)} %copy.6.counts, s32[16]{0:T(128)} %idx.1), custom_call_target="tpu_custom_call" | custom-call | tf_op jit(solution)/shard_map/pallas_call | solution.py:419
  50.0 1.4 %copy.7 = f32[16,4,128]{2,1,0:T(4,128)} copy(f32[16,4,128]{2,1,0:T(4,128)} %shard_map.46) | data formatting | bytes 65536

commit v9 on v8

--- a/solution.py
+++ b/solution.py
@@ -195,8 +195,6 @@
 
     barrier = pltpu.get_barrier_semaphore()
     peers = [near_peer, far_peer, *z_peers, *reduction_peers()]
-    for peer in peers:
-        pl.semaphore_signal(barrier, inc=1, device_id=peer, device_id_type=MESH)
     small = [pltpu.make_async_copy(weights, weights_in, local_sem.at[6])]
     copies = []
     for c in range(3):
@@ -209,6 +207,8 @@
             )
     for copy in (*small, *copies):
         copy.start()
+    for peer in peers:
+        pl.semaphore_signal(barrier, inc=1, device_id=peer, device_id_type=MESH)
     for c in range(3):
         for side in range(2):
             planes[c, side, pl.ds(0, PAD), :] = jnp.zeros((PAD, M), BF)
@@ -269,11 +269,12 @@
     lax.fori_loop(0, 8, send_edges, 0)
     pl.semaphore_wait(barrier, len(peers))
     for t in range(8):
-        near_copy(lax.rem(t + 4 * odd, 8)).start()
         z_copy(0, block_of(t)).start()
         z_copy(1, block_of(t)).start()
     for p in range(4):
         far_copy(p).start()
+    for t in range(8):
+        near_copy(lax.rem(t + 4 * odd, 8)).start()
     weight_copy.start()
     for k in range(8):
         for side in range(2):

time: 51.5 us -> 51.6 us (level)
  no operation moved by 1% of the time
where the time goes in v9:
time: 51.6 us; the launch traced here: 51.4 us
  Pallas kernels  49.3 us (96%)
  local copies, waits for them, and re-layouts  1.38 us (3%)
  between operations  0.66 us (1%)
    pallas_call x1, Pallas kernels, local(): pl.pallas_call(local_kernel, out_shape=jax.ShapeDtypeStruct((JW, 4, M), F...  49.3 us
    unnamed x1, local copies, waits for them, and re-layouts  1.38 us

profile of v9, /device:TPU:1, one launch (start us, length us, event | category | flops | bytes accessed | tf_op | source)
XLA Modules:
  0.0 51.4 jit_solution(4818154658000584434)
XLA Ops:
  0.7 49.3 %shard_map.46 = f32[16,4,128]{2,1,0:T(4,128)} custom-call(bf16[3,2,1024,128]{3,2,1,0:T(8,128)(2,1)} %bitcast.2, f32[2,8,128]{2,1,0:T(8,128)} %bitcast.3, s32[1]{0:T(128)S(6)} %copy.6.counts, s32[16]{0:T(128)} %idx.1), custom_call_target="tpu_custom_call" | custom-call | tf_op jit(solution)/shard_map/pallas_call | solution.py:420
  50.0 1.4 %copy.7 = f32[16,4,128]{2,1,0:T(4,128)} copy(f32[16,4,128]{2,1,0:T(4,128)} %shard_map.46) | data formatting | bytes 65536
